TPU v7x, 32 devices: a whole 2x2x4 slice. The times are simulated.
32 devices in a mesh: dom: 16 (over z, y, x), feat: 2 (over core).
Axes of the slice: x: 2, y: 2, z: 4, core: 2. Of those that a mesh axis runs over, the one named last changes fastest.
Arguments:
- features: bfloat16 [32768, 608], P('dom', 'feat'), may hold values from -6 to 6
- weight: bfloat16 [608, 256], replicated, may hold values from -0.25 to 0.25
- out_bias: float32 [256], P('feat'), may hold values from -3 to 3
- tile_values: bfloat16 [1728, 128, 128], P('dom'), may hold values from -0.25 to 0.25
- tile_rows: int32 [1728], P('dom'), may hold values from 0 to 15
- tile_cols: int32 [1728], P('dom'), may hold values from 0 to 81, as said below
- tile_count: int32 [16], P('dom'), may hold values from 10 to 108, as said below
- send_rows: int32 [16, 8, 1024], P('dom'), may hold values from 0 to 2047
- hub_ids: int32 [256], replicated, may hold values from 0 to 32767, as said below
Outputs:
- activations: bfloat16 [32768, 256], P('dom', 'feat')
Inputs may be any that keep to these rules, and one draw needn't show every extreme that they name: `tile_count`: slots at or past a partition's count are not part of the graph; some partition uses all 108 slots. `tile_cols`: column blocks index the extended row space of the slot's partition. `hub_ids`: distinct vertex ids; vertex v belongs to partition v // 2048; no partition owns more than 48 hubs, and some partition owns exactly 48.
All inputs are finite; a program needn't handle non-finite values.
Results may differ from a plain program's by a relative error of at most 0.0044.
Values may be sent and summed in bfloat16 or wider, within the bound.
No kernel may reach another device: no remote copies, remote signals or barrier semaphores. Data moves between devices by JAX's collectives and lax.ppermute only.
A program may use at most 64 MiB of HBM per device.

v0:
```python
import functools

import jax
import jax.numpy as jnp
from jax import lax
from jax.experimental import pallas as pl
from jax.experimental.pallas import tpu as pltpu
from jax.sharding import PartitionSpec as P


UNROLL = 4
FOLDS = 4
ORDER = ((5, 4), (2, 3), (6, 7), (1, 0))


def passed_along(value, axis, steps):
    count = lax.axis_size(axis)
    initial, last = (max(0, -steps), min(count, count - steps))
    return lax.ppermute(value, axis, [(source, source + steps) for source in range(initial, last)])


def exchanged(value, axis, step):
    count = lax.axis_size(axis)
    return lax.ppermute(value, axis, [(i, i ^ step) for i in range(count)])


def send_order(reach):
    if reach == 4:
        return ORDER
    return tuple((k, 2 * reach - 1 - k) for k in range(reach))


def project_kernel(local_hubs, *refs, parts):
    features = refs[:parts]
    weights = refs[parts : 2 * parts]
    folded, rows_bf16, hub_part = refs[2 * parts :]
    total = None
    for feature, weight in zip(features, weights):
        piece = lax.dot_general(
            weight[...], feature[...], (((0,), (0,)), ((), ())), preferred_element_type=jnp.float32
        )
        total = piece if total is None else total + piece
    rounded = total.T.astype(jnp.bfloat16)
    rows_bf16[...] = rounded
    depth, width = folded.shape[0], rounded.shape[1]
    for k in range(folded.shape[1] // width):
        folded[:, k * width : (k + 1) * width] = rounded[k * depth : (k + 1) * depth]
    chunk = 256
    ids = local_hubs[...]
    picked = jnp.zeros(hub_part.shape, jnp.float32)
    for start in range(0, rounded.shape[0], chunk):
        lanes = lax.broadcasted_iota(jnp.int32, (ids.shape[0], chunk), 1) + start
        chosen = jnp.where(ids == lanes, 1.0, 0.0).astype(jnp.bfloat16)
        picked += jnp.dot(
            chosen, rounded[start : start + chunk], preferred_element_type=jnp.float32
        )
    hub_part[...] = picked.astype(jnp.bfloat16)


def pick_kernel(send_rows, folded, *refs, slots, with_hubs):
    outs = refs[-len(slots) :]
    if with_hubs:
        mine, theirs, summed = refs[:3]
        summed[...] = mine[...] + theirs[...]
    depth, total_width = folded.shape
    source = folded[...]
    turned = send_rows[...].T
    piece = 256
    for slot, out in zip(slots, outs):
        width = out.shape[1]
        for start in range(0, out.shape[0], piece):
            ids = turned[start : start + piece, slot : slot + 1]
            lanes = lax.broadcasted_iota(jnp.int32, (piece, depth), 1)
            chosen = jnp.where((ids & (depth - 1)) == lanes, 1.0, 0.0).astype(jnp.bfloat16)
            wide = jnp.dot(chosen, source, preferred_element_type=jnp.float32)
            picked = wide[:, :width]
            for k in range(1, total_width // width):
                picked = jnp.where(ids >= k * depth, wide[:, k * width : (k + 1) * width], picked)
            out[start : start + piece] = picked.astype(jnp.bfloat16)


def listed(rows, cols, count, chosen, first, last, spare):
    chosen_slot, chosen_row, chosen_col = chosen

    def step(t, n):
        col = cols[t]
        chosen_slot[n] = t
        chosen_row[n] = rows[t]
        chosen_col[n] = col
        return n + jnp.where((col >= first) & (col < last), 1, 0)

    n = lax.fori_loop(0, count[0], step, jnp.int32(0))
    for j in range(UNROLL):
        chosen_slot[n + j] = 0
        chosen_row[n + j] = spare
        chosen_col[n + j] = first
    return n


def add_products(n, chosen, tiles, ext, base, acc):
    chosen_slot, chosen_row, chosen_col = chosen
    edge = tiles.shape[1]

    @pl.loop(0, (n + UNROLL - 1) // UNROLL)
    def _(group):
        products = []
        for j in range(UNROLL):
            k = group * UNROLL + j
            start = pl.multiple_of((chosen_col[k] - base) * edge, edge)
            products.append(
                jnp.dot(
                    tiles[chosen_slot[k]],
                    ext[pl.ds(start, edge), :],
                    preferred_element_type=jnp.float32,
                )
            )
        for j in range(UNROLL):
            row = chosen_row[group * UNROLL + j]
            acc[row] += products[j]


def own_kernel(rows, cols, count, tiles, own, acc, *chosen):
    blocks = acc.shape[0] - 1
    acc[...] = jnp.zeros(acc.shape, jnp.float32)
    n = listed(rows, cols, count, chosen, 0, own.shape[0] // tiles.shape[1], blocks)
    add_products(n, chosen, tiles, own, 0, acc)


def rest_kernel(rows, cols, count, bias, tiles, acc_in, *refs):
    sources = refs[:-7]
    out, ext, acc, sems = refs[-7:-3]
    chosen = refs[-3:]
    edge = tiles.shape[1]
    copies, start = [], 0
    for k, source in enumerate(sources):
        copies.append(
            pltpu.make_async_copy(source, ext.at[pl.ds(start, source.shape[0]), :], sems.at[k])
        )
        start += source.shape[0]
        copies[-1].start()
    blocks = acc.shape[0] - 1
    first = blocks
    acc[...] = acc_in[...]
    n = listed(rows, cols, count, chosen, first, first + start // edge, blocks)
    for copy in copies:
        copy.wait()
    add_products(n, chosen, tiles, ext, first, acc)
    total = acc[:blocks].reshape(out.shape)
    out[...] = jnp.maximum(total + bias[...], 0.0).astype(jnp.bfloat16)


def local(
    features, weight, out_bias, tile_values, tile_rows, tile_cols, tile_count, send_rows, hub_ids
):
    column_count = out_bias.shape[0]
    vertex_rows, feature_count = features.shape
    part_index = lax.axis_index("dom")
    feat_index = lax.axis_index("feat")
    feat_size = lax.axis_size("feat")
    part_count = lax.axis_size("dom")
    slot_total, half_rows = send_rows.shape[1:]
    reach = slot_total // 2
    offsets = list(range(-reach, 0)) + list(range(1, reach + 1))
    edge = tile_values.shape[1]
    blocks = vertex_rows // edge
    hub_total = hub_ids.shape[0]
    smem = pl.BlockSpec(memory_space=pltpu.SMEM)
    vmem = pl.BlockSpec(memory_space=pltpu.VMEM)
    hbm = pl.BlockSpec(memory_space=pl.ANY)

    turned = features.T
    feature_parts, weight_parts = [], []
    for shift in range(feat_size):
        piece = turned
        if shift:
            ring = [(i, (i + shift) % feat_size) for i in range(feat_size)]
            piece = lax.ppermute(turned, "feat", ring)
        origin = (feat_index - shift) % feat_size
        feature_parts.append(piece)
        weight_parts.append(
            lax.dynamic_slice(
                weight,
                (origin * feature_count, feat_index * column_count),
                (feature_count, column_count),
            )
        )
    local_hubs = (hub_ids - part_index * vertex_rows).reshape(hub_total, 1)
    folds = FOLDS if column_count % 128 == 0 else 1
    depth = vertex_rows // folds
    assert depth & (depth - 1) == 0
    folded, rows_bf16, hub_part = pl.pallas_call(
        functools.partial(project_kernel, parts=feat_size),
        out_shape=(
            jax.ShapeDtypeStruct((depth, folds * column_count), jnp.bfloat16),
            jax.ShapeDtypeStruct((vertex_rows, column_count), jnp.bfloat16),
            jax.ShapeDtypeStruct((hub_total, column_count), jnp.bfloat16),
        ),
        in_specs=[vmem] * (1 + 2 * feat_size),
        out_specs=[vmem] * 3,
        name="project",
    )(local_hubs, *feature_parts, *weight_parts)
    steps = []
    while 1 << len(steps) < part_count:
        steps.append(1 << len(steps))
    assert part_count == 1 << len(steps)
    hub_mine, hub_theirs, stage = hub_part, None, 0

    def start_stage():
        nonlocal hub_theirs, stage
        if stage < len(steps):
            hub_theirs = exchanged(hub_mine, "dom", steps[stage])
            stage += 1
        else:
            hub_theirs = None

    start_stage()
    received = [None] * slot_total
    row_type = jax.ShapeDtypeStruct((half_rows, column_count), jnp.bfloat16)
    hub_type = jax.ShapeDtypeStruct((hub_total, column_count), jnp.bfloat16)
    for group, slots in enumerate(send_order(reach)):
        hubs = group > 0 and hub_theirs is not None
        picked = pl.pallas_call(
            functools.partial(pick_kernel, slots=slots, with_hubs=hubs),
            out_shape=[hub_type] * hubs + [row_type] * len(slots),
            in_specs=[vmem] * (2 + 2 * hubs),
            out_specs=[vmem] * (hubs + len(slots)),
            name="pick_rows",
        )(send_rows[0], folded, *([hub_mine, hub_theirs] if hubs else []))
        if hubs:
            hub_mine = picked[0]
            start_stage()
        for slot, rows in zip(slots, picked[hubs:]):
            received[slot] = passed_along(rows, "dom", offsets[slot])
    while hub_theirs is not None:
        hub_mine = hub_mine + hub_theirs
        start_stage()
    hub_block = hub_mine

    lists = [pltpu.SMEM((tile_values.shape[0] + UNROLL,), jnp.int32)] * 3
    acc_shape = (blocks + 1, edge, column_count)
    partial_sum = pl.pallas_call(
        own_kernel,
        out_shape=jax.ShapeDtypeStruct(acc_shape, jnp.float32),
        in_specs=[smem] * 3 + [vmem] * 2,
        out_specs=vmem,
        scratch_shapes=lists,
        name="own_tiles",
    )(tile_rows, tile_cols, tile_count, tile_values, rows_bf16)
    sources = received + [hub_block]
    ext_rows = sum(source.shape[0] for source in sources)
    return pl.pallas_call(
        rest_kernel,
        out_shape=jax.ShapeDtypeStruct((vertex_rows, column_count), jnp.bfloat16),
        in_specs=[smem] * 3 + [vmem] * 3 + [hbm] * len(sources),
        out_specs=vmem,
        scratch_shapes=[
            pltpu.VMEM((ext_rows, column_count), jnp.bfloat16),
            pltpu.VMEM(acc_shape, jnp.float32),
            pltpu.SemaphoreType.DMA((len(sources),)),
        ]
        + lists,
        name="other_tiles",
    )(
        tile_rows,
        tile_cols,
        tile_count,
        out_bias.reshape(1, column_count),
        tile_values,
        partial_sum,
        *sources,
    )


def solution(mesh):
    in_specs = (
        P("dom", "feat"),
        P(),
        P("feat"),
        P("dom", None, None),
        P("dom"),
        P("dom"),
        P("dom"),
        P("dom", None, None),
        P(),
    )
    out_specs = P("dom", "feat")
    return jax.shard_map(local, mesh=mesh, in_specs=in_specs, out_specs=out_specs, check_vma=False)
```

profile of v0, /device:TPU:2, one launch (start us, length us, event | category | flops | bytes accessed | tf_op | source)
XLA Modules:
  0.0 83.4 jit_solution(14705132527673241441)
XLA Ops:
  0.0 0.0 collective-permute-start
  0.0 0.7 broadcast_subtract_fusion
  0.7 0.8 copy.10.local_hubs
  1.5 1.6 %fusion = (bf16[304,128]{1,0:T(8,128)(2,1)}, bf16[304,128]{1,0:T(8,128)(2,1)}) fusion(bf16[608,256]{1,0:T(8,128)(2,1)} %param.10, s32[]{:T(128)S(6)} %select_n.25, s32[]{:T(128)S(6)} %select_n.23, s32[]{:T(128)S(6)} %select_n.22), kind=kLoop, calls=%fused_computation.1 | loop fusion | bytes 311308 | tf_op jit(solution)/shard_map/dynamic_slice | solution.py:181
  3.1 0.1 collective-permute-done.refs_1_
  3.2 0.0 copy-start
  3.2 1.1 %copy-done = bf16[304,2048]{1,0:T(8,128)(2,1)} copy-done((bf16[304,2048]{1,0:T(8,128)(2,1)}, bf16[304,2048]{1,0:T(8,128)(2,1)S(1)}, u32[]{:S(2)}) %copy-start) | copy-done | bytes 1245208
  4.2 3.6 %project.1 = (bf16[512,512]{1,0:T(8,128)(2,1)}, bf16[2048,128]{1,0:T(8,128)(2,1)}, bf16[256,128]{1,0:T(8,128)(2,1)}) custom-call(s32[256,1]{1,0:T(8,128)} %copy.10.local_hubs, bf16[304,2048]{1,0:T(8,128)(2,1)} %bitcast.5, bf16[304,2048]{1,0:T(8,128)(2,1)} %copy-done, bf16[304,128]{1,0:T(8,128)(2,1)} %get-tuple-element.34.refs_2_, ...), custom_call_target="tpu_custom_call" | custom-call | tf_op jit(solution)/shard_map/project/pallas_call | solution.py:191
  7.8 0.0 collective-permute-start.1
  7.8 3.3 %pick_rows.7 = (bf16[1024,128]{1,0:T(8,128)(2,1)}, bf16[1024,128]{1,0:T(8,128)(2,1)}) custom-call(s32[8,1024]{1,0:T(8,128)} %bitcast.6, bf16[512,512]{1,0:T(8,128)(2,1)} %get-tuple-element.20.folded), custom_call_target="tpu_custom_call" | custom-call | tf_op jit(solution)/shard_map/pick_rows/pallas_call | solution.py:222
  11.1 4.9 %collective-permute-start.8 = (bf16[1024,128]{1,0:T(8,128)(2,1)}, bf16[1024,128]{1,0:T(8,128)(2,1)S(1)}, u32[]{:S(2)}, u32[]{:S(2)}) collective-permute-start(bf16[1024,128]{1,0:T(8,128)(2,1)} %get-tuple-element.28), channel_id=1, source_target_pairs={{0,2},{2,4},{4,6},{6,8},{8,10},{10,12},{12,14},{14,16},{16,18},{18... | collective-permute-start | bytes 786440 | tf_op jit(solution)/shard_map/ppermute | solution.py:19
  16.0 3.4 %collective-permute-start.9 = (bf16[1024,128]{1,0:T(8,128)(2,1)}, bf16[1024,128]{1,0:T(8,128)(2,1)S(1)}, u32[]{:S(2)}, u32[]{:S(2)}) collective-permute-start(bf16[1024,128]{1,0:T(8,128)(2,1)} %get-tuple-element.29), channel_id=1, source_target_pairs={{0,4},{2,6},{4,8},{6,10},{8,12},{10,14},{12,16},{14,18},{16,20},{1... | collective-permute-start | bytes 786440 | tf_op jit(solution)/shard_map/ppermute | solution.py:19
  19.4 0.0 collective-permute-done.1.refs_1_
  19.4 0.0 copy-start.10
  19.5 0.6 copy-done.10
  20.1 3.3 %pick_rows.4 = (bf16[256,128]{1,0:T(8,128)(2,1)}, bf16[1024,128]{1,0:T(8,128)(2,1)}, bf16[1024,128]{1,0:T(8,128)(2,1)}) custom-call(s32[8,1024]{1,0:T(8,128)} %bitcast.7, bf16[512,512]{1,0:T(8,128)(2,1)} %get-tuple-element.20.folded, bf16[256,128]{1,0:T(8,128)(2,1)} %get-tuple-element.21.refs_0_, bf16[256,128]{1,0:T(8,128)(2,1)} %copy-done.10), custom_call_target="tpu_custom_call" | custom-call | tf_op jit(solution)/shard_map/pick_rows/pallas_call | solution.py:222
  23.4 0.0 copy-start.13
  23.4 1.4 %collective-permute-start.6 = (bf16[1024,128]{1,0:T(8,128)(2,1)}, bf16[1024,128]{1,0:T(8,128)(2,1)S(1)}, u32[]{:S(2)}, u32[]{:S(2)}) collective-permute-start(bf16[1024,128]{1,0:T(8,128)(2,1)} %get-tuple-element.26), channel_id=1, source_target_pairs={{4,0},{6,2},{8,4},{10,6},{12,8},{14,10},{16,12},{18,14},{20,16},{2... | collective-permute-start | bytes 786440 | tf_op jit(solution)/shard_map/ppermute | solution.py:19
  24.8 2.7 %collective-permute-start.2 = (bf16[256,128]{1,0:T(8,128)(2,1)}, bf16[256,128]{1,0:T(8,128)(2,1)S(1)}, u32[]{:S(2)}, u32[]{:S(2)}) collective-permute-start(bf16[256,128]{1,0:T(8,128)(2,1)} %get-tuple-element.22.refs_0_), channel_id=1, source_target_pairs={{0,4},{2,6},{4,0},{6,2},{8,12},{10,14},{12,8},{14,10},{16,20},{18,... | collective-permute-start | bytes 196616 | tf_op jit(solution)/shard_map/ppermute | solution.py:24
  27.5 7.3 %collective-permute-done.2.refs_1_ = bf16[256,128]{1,0:T(8,128)(2,1)S(1)} collective-permute-done((bf16[256,128]{1,0:T(8,128)(2,1)}, bf16[256,128]{1,0:T(8,128)(2,1)S(1)}, u32[]{:S(2)}, u32[]{:S(2)}) %collective-permute-start.2) | collective-permute-done | bytes 65568 | tf_op jit(solution)/shard_map/ppermute | solution.py:24
  34.8 0.0 copy-start.12
  34.8 0.6 copy-done.12
  35.4 3.3 %pick_rows.5 = (bf16[256,128]{1,0:T(8,128)(2,1)}, bf16[1024,128]{1,0:T(8,128)(2,1)}, bf16[1024,128]{1,0:T(8,128)(2,1)}) custom-call(s32[8,1024]{1,0:T(8,128)} %bitcast.8, bf16[512,512]{1,0:T(8,128)(2,1)} %get-tuple-element.20.folded, bf16[256,128]{1,0:T(8,128)(2,1)} %get-tuple-element.22.refs_0_, bf16[256,128]{1,0:T(8,128)(2,1)} %copy-done.12), custom_call_target="tpu_custom_call" | custom-call | tf_op jit(solution)/shard_map/pick_rows/pallas_call | solution.py:222
  38.7 4.7 %collective-permute-start.3 = (bf16[256,128]{1,0:T(8,128)(2,1)}, bf16[256,128]{1,0:T(8,128)(2,1)S(1)}, u32[]{:S(2)}, u32[]{:S(2)}) collective-permute-start(bf16[256,128]{1,0:T(8,128)(2,1)} %get-tuple-element.23.refs_0_), channel_id=1, source_target_pairs={{0,8},{2,10},{4,12},{6,14},{8,0},{10,2},{12,4},{14,6},{16,24},{18,... | collective-permute-start | bytes 196616 | tf_op jit(solution)/shard_map/ppermute | solution.py:24
  43.4 2.5 %collective-permute-done.3.refs_1_ = bf16[256,128]{1,0:T(8,128)(2,1)S(1)} collective-permute-done((bf16[256,128]{1,0:T(8,128)(2,1)}, bf16[256,128]{1,0:T(8,128)(2,1)S(1)}, u32[]{:S(2)}, u32[]{:S(2)}) %collective-permute-start.3) | collective-permute-done | bytes 65568 | tf_op jit(solution)/shard_map/ppermute | solution.py:24
  45.8 0.6 copy-done.11
  46.5 3.3 %pick_rows.6 = (bf16[256,128]{1,0:T(8,128)(2,1)}, bf16[1024,128]{1,0:T(8,128)(2,1)}, bf16[1024,128]{1,0:T(8,128)(2,1)}) custom-call(s32[8,1024]{1,0:T(8,128)} %bitcast.9, bf16[512,512]{1,0:T(8,128)(2,1)} %get-tuple-element.20.folded, bf16[256,128]{1,0:T(8,128)(2,1)} %get-tuple-element.23.refs_0_, bf16[256,128]{1,0:T(8,128)(2,1)} %copy-done.11), custom_call_target="tpu_custom_call" | custom-call | tf_op jit(solution)/shard_map/pick_rows/pallas_call | solution.py:222
  49.8 3.0 %collective-permute-start.12 = (bf16[256,128]{1,0:T(8,128)(2,1)}, bf16[256,128]{1,0:T(8,128)(2,1)S(1)}, u32[]{:S(2)}, u32[]{:S(2)}) collective-permute-start(bf16[256,128]{1,0:T(8,128)(2,1)} %get-tuple-element.32), channel_id=1, source_target_pairs={{0,16},{2,18},{4,20},{6,22},{8,24},{10,26},{12,28},{14,30},{16,0},... | collective-permute-start | bytes 196616 | tf_op jit(solution)/shard_map/ppermute | solution.py:24
  52.8 0.0 copy-done.13
  52.8 2.0 %collective-permute-start.7 = (bf16[1024,128]{1,0:T(8,128)(2,1)S(1)}, bf16[1024,128]{1,0:T(8,128)(2,1)S(1)}, u32[]{:S(2)}, u32[]{:S(2)}) collective-permute-start(bf16[1024,128]{1,0:T(8,128)(2,1)S(1)} %copy-done.13), channel_id=1, source_target_pairs={{2,0},{4,2},{6,4},{8,6},{10,8},{12,10},{14,12},{16,14},{18,16},{20... | collective-permute-start | bytes 786440 | tf_op jit(solution)/shard_map/ppermute | solution.py:19
  54.8 0.0 collective-permute-done.8.refs_4_
  54.8 0.0 copy-start.1
  54.8 3.8 %collective-permute-start.10 = (bf16[1024,128]{1,0:T(8,128)(2,1)}, bf16[1024,128]{1,0:T(8,128)(2,1)S(1)}, u32[]{:S(2)}, u32[]{:S(2)}) collective-permute-start(bf16[1024,128]{1,0:T(8,128)(2,1)} %get-tuple-element.30), channel_id=1, source_target_pairs={{0,6},{2,8},{4,10},{6,12},{8,14},{10,16},{12,18},{14,20},{16,22},{... | collective-permute-start | bytes 786440 | tf_op jit(solution)/shard_map/ppermute | solution.py:19
  58.6 0.0 collective-permute-done.9.refs_5_
  58.6 0.0 copy-start.2
  58.6 3.5 %collective-permute-start.11 = (bf16[1024,128]{1,0:T(8,128)(2,1)}, bf16[1024,128]{1,0:T(8,128)(2,1)S(1)}, u32[]{:S(2)}, u32[]{:S(2)}) collective-permute-start(bf16[1024,128]{1,0:T(8,128)(2,1)} %get-tuple-element.31), channel_id=1, source_target_pairs={{0,8},{2,10},{4,12},{6,14},{8,16},{10,18},{12,20},{14,22},{16,24},... | collective-permute-start | bytes 786440 | tf_op jit(solution)/shard_map/ppermute | solution.py:19
  62.2 0.0 collective-permute-done.12
  62.2 1.3 %collective-permute-start.4 = (bf16[1024,128]{1,0:T(8,128)(2,1)}, bf16[1024,128]{1,0:T(8,128)(2,1)S(1)}, u32[]{:S(2)}, u32[]{:S(2)}) collective-permute-start(bf16[1024,128]{1,0:T(8,128)(2,1)} %get-tuple-element.24), channel_id=1, source_target_pairs={{8,0},{10,2},{12,4},{14,6},{16,8},{18,10},{20,12},{22,14},{24,16},... | collective-permute-start | bytes 786440 | tf_op jit(solution)/shard_map/ppermute | solution.py:19
  63.5 0.0 collective-permute-done.6.refs_2_
  63.5 0.0 copy-start.3
  63.5 1.3 %collective-permute-start.5 = (bf16[1024,128]{1,0:T(8,128)(2,1)}, bf16[1024,128]{1,0:T(8,128)(2,1)S(1)}, u32[]{:S(2)}, u32[]{:S(2)}) collective-permute-start(bf16[1024,128]{1,0:T(8,128)(2,1)} %get-tuple-element.25), channel_id=1, source_target_pairs={{6,0},{8,2},{10,4},{12,6},{14,8},{16,10},{18,12},{20,14},{22,16},{... | collective-permute-start | bytes 786440 | tf_op jit(solution)/shard_map/ppermute | solution.py:19
  65.4 0.0 copy-start.9
  65.4 4.4 %own_tiles.1.acc_in = f32[17,128,128]{2,1,0:T(8,128)} custom-call(s32[108]{0:T(128)} %rows.3, s32[108]{0:T(128)} %cols.3, s32[1]{0:T(128)S(6)} %copy.11.count, bf16[108,128,128]{2,1,0:T(8,128)(2,1)} %tiles.3, bf16[2048,128]{1,0:T(8,128)(2,1)} %get-tuple-element.19.own), custom_call_target="tpu_custom_call" | custom-call | tf_op jit(solution)/shard_map/own_tiles/pallas_call | solution.py:241
  69.8 0.0 copy-done.1
  69.8 0.0 copy-done.2
  69.8 0.0 copy-done.3
  69.8 0.0 copy-done.9
  69.8 0.7 add.26.refs_8_
  70.5 0.0 collective-permute-done.7.refs_3_
  70.5 0.0 copy-start.4
  70.5 0.0 collective-permute-done.10.refs_6_
  70.5 0.0 copy-start.5
  70.5 0.0 collective-permute-done.11.refs_7_
  70.5 0.0 copy-start.6
  70.5 2.5 %collective-permute-done.4.refs_0_ = bf16[1024,128]{1,0:T(8,128)(2,1)S(1)} collective-permute-done((bf16[1024,128]{1,0:T(8,128)(2,1)}, bf16[1024,128]{1,0:T(8,128)(2,1)S(1)}, u32[]{:S(2)}, u32[]{:S(2)}) %collective-permute-start.4) | collective-permute-done | bytes 262176 | tf_op jit(solution)/shard_map/ppermute | solution.py:19
  73.0 0.0 copy-start.7
  73.0 1.9 %collective-permute-done.5.refs_1_ = bf16[1024,128]{1,0:T(8,128)(2,1)S(1)} collective-permute-done((bf16[1024,128]{1,0:T(8,128)(2,1)}, bf16[1024,128]{1,0:T(8,128)(2,1)S(1)}, u32[]{:S(2)}, u32[]{:S(2)}) %collective-permute-start.5) | collective-permute-done | bytes 262176 | tf_op jit(solution)/shard_map/ppermute | solution.py:19
  74.9 0.0 copy-start.8
  74.9 0.0 copy-done.4
  74.9 0.0 copy-done.5
  74.9 0.0 copy-done.6
  74.9 0.0 copy-done.7
  74.9 0.7 copy-done.8
  75.6 7.8 %other_tiles.1 = bf16[2048,128]{1,0:T(8,128)(2,1)} custom-call(s32[108]{0:T(128)} %rows.3, s32[108]{0:T(128)} %cols.3, s32[1]{0:T(128)S(6)} %copy.11.count, f32[1,128]{1,0:T(1,128)} %bitcast.11, bf16[108,128,128]{2,1,0:T(8,128)(2,1)} %tiles.3, f32[17,128,128]{2,1,0:T(8,128)} %own_tiles.1.acc_in, bf16[1024,128]{1,0:T(8,128)(2,1)} %copy-done.7, ...), custom_call_target="tpu_custom_call" | custom-call | tf_op jit(solution)/shard_map/other_tiles/pallas_call | solution.py:251
  (1 shorter events, 0.0 us)
Async XLA Ops:
  0.0 3.2 %collective-permute-start = (bf16[304,2048]{1,0:T(8,128)(2,1)}, bf16[304,2048]{1,0:T(8,128)(2,1)S(1)}, u32[]{:S(2)}, u32[]{:S(2)}) collective-permute-start(bf16[304,2048]{1,0:T(8,128)(2,1)} %bitcast.4), channel_id=1, source_target_pairs={{0,1},{1,0},{2,3},{3,2},{4,5},{5,4},{6,7},{7,6},{8,9},{9,8},{10,11... | collective-permute-start | bytes 3735560 | tf_op jit(solution)/shard_map/ppermute | solution.py:177
  3.2 1.1 %copy-start = (bf16[304,2048]{1,0:T(8,128)(2,1)}, bf16[304,2048]{1,0:T(8,128)(2,1)S(1)}, u32[]{:S(2)}) copy-start(bf16[304,2048]{1,0:T(8,128)(2,1)S(1)} %collective-permute-done.refs_1_) | copy-start | bytes 3735556
  7.8 11.7 %collective-permute-start.1 = (bf16[256,128]{1,0:T(8,128)(2,1)}, bf16[256,128]{1,0:T(8,128)(2,1)S(1)}, u32[]{:S(2)}, u32[]{:S(2)}) collective-permute-start(bf16[256,128]{1,0:T(8,128)(2,1)} %get-tuple-element.21.refs_0_), channel_id=1, source_target_pairs={{0,2},{2,0},{4,6},{6,4},{8,10},{10,8},{12,14},{14,12},{16,18},{18,... | collective-permute-start | bytes 196616 | tf_op jit(solution)/shard_map/ppermute | solution.py:24
  11.1 43.7 %collective-permute-start.8 = (bf16[1024,128]{1,0:T(8,128)(2,1)}, bf16[1024,128]{1,0:T(8,128)(2,1)S(1)}, u32[]{:S(2)}, u32[]{:S(2)}) collective-permute-start(bf16[1024,128]{1,0:T(8,128)(2,1)} %get-tuple-element.28), channel_id=1, source_target_pairs={{0,2},{2,4},{4,6},{6,8},{8,10},{10,12},{12,14},{14,16},{16,18},{18... | collective-permute-start | bytes 786440 | tf_op jit(solution)/shard_map/ppermute | solution.py:19
  16.0 42.6 %collective-permute-start.9 = (bf16[1024,128]{1,0:T(8,128)(2,1)}, bf16[1024,128]{1,0:T(8,128)(2,1)S(1)}, u32[]{:S(2)}, u32[]{:S(2)}) collective-permute-start(bf16[1024,128]{1,0:T(8,128)(2,1)} %get-tuple-element.29), channel_id=1, source_target_pairs={{0,4},{2,6},{4,8},{6,10},{8,12},{10,14},{12,16},{14,18},{16,20},{1... | collective-permute-start | bytes 786440 | tf_op jit(solution)/shard_map/ppermute | solution.py:19
  19.4 0.6 copy-start.10
  23.4 29.4 %copy-start.13 = (bf16[1024,128]{1,0:T(8,128)(2,1)S(1)}, bf16[1024,128]{1,0:T(8,128)(2,1)}, u32[]{:S(2)}) copy-start(bf16[1024,128]{1,0:T(8,128)(2,1)} %get-tuple-element.27) | copy-start | bytes 786436
  23.4 40.1 %collective-permute-start.6 = (bf16[1024,128]{1,0:T(8,128)(2,1)}, bf16[1024,128]{1,0:T(8,128)(2,1)S(1)}, u32[]{:S(2)}, u32[]{:S(2)}) collective-permute-start(bf16[1024,128]{1,0:T(8,128)(2,1)} %get-tuple-element.26), channel_id=1, source_target_pairs={{4,0},{6,2},{8,4},{10,6},{12,8},{14,10},{16,12},{18,14},{20,16},{2... | collective-permute-start | bytes 786440 | tf_op jit(solution)/shard_map/ppermute | solution.py:19
  24.8 10.0 %collective-permute-start.2 = (bf16[256,128]{1,0:T(8,128)(2,1)}, bf16[256,128]{1,0:T(8,128)(2,1)S(1)}, u32[]{:S(2)}, u32[]{:S(2)}) collective-permute-start(bf16[256,128]{1,0:T(8,128)(2,1)} %get-tuple-element.22.refs_0_), channel_id=1, source_target_pairs={{0,4},{2,6},{4,0},{6,2},{8,12},{10,14},{12,8},{14,10},{16,20},{18,... | collective-permute-start | bytes 196616 | tf_op jit(solution)/shard_map/ppermute | solution.py:24
  34.8 0.6 copy-start.12
  38.7 7.2 %collective-permute-start.3 = (bf16[256,128]{1,0:T(8,128)(2,1)}, bf16[256,128]{1,0:T(8,128)(2,1)S(1)}, u32[]{:S(2)}, u32[]{:S(2)}) collective-permute-start(bf16[256,128]{1,0:T(8,128)(2,1)} %get-tuple-element.23.refs_0_), channel_id=1, source_target_pairs={{0,8},{2,10},{4,12},{6,14},{8,0},{10,2},{12,4},{14,6},{16,24},{18,... | collective-permute-start | bytes 196616 | tf_op jit(solution)/shard_map/ppermute | solution.py:24
  45.8 0.6 copy-start.11
  49.8 12.4 %collective-permute-start.12 = (bf16[256,128]{1,0:T(8,128)(2,1)}, bf16[256,128]{1,0:T(8,128)(2,1)S(1)}, u32[]{:S(2)}, u32[]{:S(2)}) collective-permute-start(bf16[256,128]{1,0:T(8,128)(2,1)} %get-tuple-element.32), channel_id=1, source_target_pairs={{0,16},{2,18},{4,20},{6,22},{8,24},{10,26},{12,28},{14,30},{16,0},... | collective-permute-start | bytes 196616 | tf_op jit(solution)/shard_map/ppermute | solution.py:24
  52.8 17.7 %collective-permute-start.7 = (bf16[1024,128]{1,0:T(8,128)(2,1)S(1)}, bf16[1024,128]{1,0:T(8,128)(2,1)S(1)}, u32[]{:S(2)}, u32[]{:S(2)}) collective-permute-start(bf16[1024,128]{1,0:T(8,128)(2,1)S(1)} %copy-done.13), channel_id=1, source_target_pairs={{2,0},{4,2},{6,4},{8,6},{10,8},{12,10},{14,12},{16,14},{18,16},{20... | collective-permute-start | bytes 786440 | tf_op jit(solution)/shard_map/ppermute | solution.py:19
  54.8 15.0 %copy-start.1 = (bf16[1024,128]{1,0:T(8,128)(2,1)}, bf16[1024,128]{1,0:T(8,128)(2,1)S(1)}, u32[]{:S(2)}) copy-start(bf16[1024,128]{1,0:T(8,128)(2,1)S(1)} %collective-permute-done.8.refs_4_) | copy-start | bytes 786436
  54.8 15.7 %collective-permute-start.10 = (bf16[1024,128]{1,0:T(8,128)(2,1)}, bf16[1024,128]{1,0:T(8,128)(2,1)S(1)}, u32[]{:S(2)}, u32[]{:S(2)}) collective-permute-start(bf16[1024,128]{1,0:T(8,128)(2,1)} %get-tuple-element.30), channel_id=1, source_target_pairs={{0,6},{2,8},{4,10},{6,12},{8,14},{10,16},{12,18},{14,20},{16,22},{... | collective-permute-start | bytes 786440 | tf_op jit(solution)/shard_map/ppermute | solution.py:19
  58.6 11.2 %copy-start.2 = (bf16[1024,128]{1,0:T(8,128)(2,1)}, bf16[1024,128]{1,0:T(8,128)(2,1)S(1)}, u32[]{:S(2)}) copy-start(bf16[1024,128]{1,0:T(8,128)(2,1)S(1)} %collective-permute-done.9.refs_5_) | copy-start | bytes 786436
  58.6 11.9 %collective-permute-start.11 = (bf16[1024,128]{1,0:T(8,128)(2,1)}, bf16[1024,128]{1,0:T(8,128)(2,1)S(1)}, u32[]{:S(2)}, u32[]{:S(2)}) collective-permute-start(bf16[1024,128]{1,0:T(8,128)(2,1)} %get-tuple-element.31), channel_id=1, source_target_pairs={{0,8},{2,10},{4,12},{6,14},{8,16},{10,18},{12,20},{14,22},{16,24},... | collective-permute-start | bytes 786440 | tf_op jit(solution)/shard_map/ppermute | solution.py:19
  62.2 10.9 %collective-permute-start.4 = (bf16[1024,128]{1,0:T(8,128)(2,1)}, bf16[1024,128]{1,0:T(8,128)(2,1)S(1)}, u32[]{:S(2)}, u32[]{:S(2)}) collective-permute-start(bf16[1024,128]{1,0:T(8,128)(2,1)} %get-tuple-element.24), channel_id=1, source_target_pairs={{8,0},{10,2},{12,4},{14,6},{16,8},{18,10},{20,12},{22,14},{24,16},... | collective-permute-start | bytes 786440 | tf_op jit(solution)/shard_map/ppermute | solution.py:19
  63.5 6.3 %copy-start.3 = (bf16[1024,128]{1,0:T(8,128)(2,1)}, bf16[1024,128]{1,0:T(8,128)(2,1)S(1)}, u32[]{:S(2)}) copy-start(bf16[1024,128]{1,0:T(8,128)(2,1)S(1)} %collective-permute-done.6.refs_2_) | copy-start | bytes 786436
  63.5 11.4 %collective-permute-start.5 = (bf16[1024,128]{1,0:T(8,128)(2,1)}, bf16[1024,128]{1,0:T(8,128)(2,1)S(1)}, u32[]{:S(2)}, u32[]{:S(2)}) collective-permute-start(bf16[1024,128]{1,0:T(8,128)(2,1)} %get-tuple-element.25), channel_id=1, source_target_pairs={{6,0},{8,2},{10,4},{12,6},{14,8},{16,10},{18,12},{20,14},{22,16},{... | collective-permute-start | bytes 786440 | tf_op jit(solution)/shard_map/ppermute | solution.py:19
  65.4 4.4 %copy-start.9 = (bf16[256,128]{1,0:T(8,128)(2,1)S(1)}, bf16[256,128]{1,0:T(8,128)(2,1)}, u32[]{:S(2)}) copy-start(bf16[256,128]{1,0:T(8,128)(2,1)} %get-tuple-element.32) | copy-start | bytes 196612
  70.5 4.4 %copy-start.4 = (bf16[1024,128]{1,0:T(8,128)(2,1)}, bf16[1024,128]{1,0:T(8,128)(2,1)S(1)}, u32[]{:S(2)}) copy-start(bf16[1024,128]{1,0:T(8,128)(2,1)S(1)} %collective-permute-done.7.refs_3_) | copy-start | bytes 786436
  70.5 4.4 %copy-start.5 = (bf16[1024,128]{1,0:T(8,128)(2,1)}, bf16[1024,128]{1,0:T(8,128)(2,1)S(1)}, u32[]{:S(2)}) copy-start(bf16[1024,128]{1,0:T(8,128)(2,1)S(1)} %collective-permute-done.10.refs_6_) | copy-start | bytes 786436
  70.5 4.4 %copy-start.6 = (bf16[1024,128]{1,0:T(8,128)(2,1)}, bf16[1024,128]{1,0:T(8,128)(2,1)S(1)}, u32[]{:S(2)}) copy-start(bf16[1024,128]{1,0:T(8,128)(2,1)S(1)} %collective-permute-done.11.refs_7_) | copy-start | bytes 786436
  73.0 1.9 %copy-start.7 = (bf16[1024,128]{1,0:T(8,128)(2,1)}, bf16[1024,128]{1,0:T(8,128)(2,1)S(1)}, u32[]{:S(2)}) copy-start(bf16[1024,128]{1,0:T(8,128)(2,1)S(1)} %collective-permute-done.4.refs_0_) | copy-start | bytes 786436
  74.9 0.7 copy-start.8
where the time goes:
time: 83.9 us; the launch traced here: 83.4 us
  starting transfers between devices  32.1 us (38%)
  Pallas kernels  28.8 us (34%)
  waiting for transfers between devices  14.2 us (17%)
  local copies, waits for them, and re-layouts  6.04 us (7%)
  other arithmetic  1.33 us (2%)
  between operations  0.86 us (1%)
    ppermute x8, starting transfers between devices, passed_along(): lax.ppermute(value, axis, [(source, source + steps) for source in range(i...  21.7 us
    pallas_call x4, Pallas kernels, local(): pl.pallas_call(functools.partial(pick_kernel, slots=slots, with_hubs=hubs...  13.1 us
    ppermute x4, starting transfers between devices, exchanged(): return lax.ppermute(value, axis, [(i, i ^ step) for i in range(count)])  10.4 us
    ppermute x4, waiting for transfers between devices, exchanged(): return lax.ppermute(value, axis, [(i, i ^ step) for i in range(count)])  9.78 us
    pallas_call x1, Pallas kernels, local(): pl.pallas_call(rest_kernel, out_shape=jax.ShapeDtypeStruct((vertex_rows,...  7.78 us
    ppermute x8, waiting for transfers between devices, passed_along(): lax.ppermute(value, axis, [(source, source + steps) for source in range(i...  4.39 us
    pallas_call x1, Pallas kernels, local(): pl.pallas_call(own_kernel, out_shape=jax.ShapeDtypeStruct(acc_shape, jnp....  4.36 us
    unnamed x28, local copies, waits for them, and re-layouts  3.64 us
  transfers between devices with their start and end apart: 13, of which 5 were waited for; matrix products, arithmetic and copies ran while one was open for 4% of the time, Pallas kernels for 21%

commit v1 on v0

--- a/solution.py
+++ b/solution.py
@@ -27,7 +27,7 @@
 def send_order(reach):
     if reach == 4:
         return ORDER
-    return tuple((k, 2 * reach - 1 - k) for k in range(reach))
+    return tuple((reach + k, reach - 1 - k) for k in range(reach))
 
 
 def project_kernel(local_hubs, *refs, parts):
@@ -79,7 +79,7 @@
             out[start : start + piece] = picked.astype(jnp.bfloat16)
 
 
-def listed(rows, cols, count, chosen, first, last, spare):
+def listed(rows, cols, count, chosen, ranges, spare):
     chosen_slot, chosen_row, chosen_col = chosen
 
     def step(t, n):
@@ -87,17 +87,20 @@
         chosen_slot[n] = t
         chosen_row[n] = rows[t]
         chosen_col[n] = col
-        return n + jnp.where((col >= first) & (col < last), 1, 0)
+        inside = jnp.int32(0)
+        for first, last in ranges:
+            inside += jnp.where((col >= first) & (col < last), 1, 0)
+        return n + inside
 
     n = lax.fori_loop(0, count[0], step, jnp.int32(0))
     for j in range(UNROLL):
         chosen_slot[n + j] = 0
         chosen_row[n + j] = spare
-        chosen_col[n + j] = first
+        chosen_col[n + j] = ranges[0][0]
     return n
 
 
-def add_products(n, chosen, tiles, ext, base, acc):
+def add_products(n, chosen, tiles, ext, acc):
     chosen_slot, chosen_row, chosen_col = chosen
     edge = tiles.shape[1]
 
@@ -106,7 +109,7 @@
         products = []
         for j in range(UNROLL):
             k = group * UNROLL + j
-            start = pl.multiple_of((chosen_col[k] - base) * edge, edge)
+            start = pl.multiple_of(chosen_col[k] * edge, edge)
             products.append(
                 jnp.dot(
                     tiles[chosen_slot[k]],
@@ -122,31 +125,40 @@
 def own_kernel(rows, cols, count, tiles, own, acc, *chosen):
     blocks = acc.shape[0] - 1
     acc[...] = jnp.zeros(acc.shape, jnp.float32)
-    n = listed(rows, cols, count, chosen, 0, own.shape[0] // tiles.shape[1], blocks)
-    add_products(n, chosen, tiles, own, 0, acc)
-
-
-def rest_kernel(rows, cols, count, bias, tiles, acc_in, *refs):
-    sources = refs[:-7]
-    out, ext, acc, sems = refs[-7:-3]
+    n = listed(rows, cols, count, chosen, ((0, blocks),), blocks)
+    add_products(n, chosen, tiles, own, acc)
+
+
+def more_kernel(rows, cols, count, bias, tiles, acc_in, *refs, starts, finish):
+    sources = refs[: len(starts)]
+    refs = refs[len(starts) :]
+    if finish:
+        out, ext, sems, acc = refs[:4]
+    else:
+        acc, ext, sems = refs[:3]
     chosen = refs[-3:]
     edge = tiles.shape[1]
-    copies, start = [], 0
-    for k, source in enumerate(sources):
+    copies, ranges = [], []
+    for k, (source, start) in enumerate(zip(sources, starts)):
+        length = source.shape[0]
         copies.append(
-            pltpu.make_async_copy(source, ext.at[pl.ds(start, source.shape[0]), :], sems.at[k])
-        )
-        start += source.shape[0]
+            pltpu.make_async_copy(source, ext.at[pl.ds(start, length), :], sems.at[k])
+        )
         copies[-1].start()
+        first, last = start // edge, (start + length) // edge
+        if ranges and ranges[-1][1] == first:
+            ranges[-1] = (ranges[-1][0], last)
+        else:
+            ranges.append((first, last))
     blocks = acc.shape[0] - 1
-    first = blocks
     acc[...] = acc_in[...]
-    n = listed(rows, cols, count, chosen, first, first + start // edge, blocks)
+    n = listed(rows, cols, count, chosen, ranges, blocks)
     for copy in copies:
         copy.wait()
-    add_products(n, chosen, tiles, ext, first, acc)
-    total = acc[:blocks].reshape(out.shape)
-    out[...] = jnp.maximum(total + bias[...], 0.0).astype(jnp.bfloat16)
+    add_products(n, chosen, tiles, ext, acc)
+    if finish:
+        total = acc[:blocks].reshape(out.shape)
+        out[...] = jnp.maximum(total + bias[...], 0.0).astype(jnp.bfloat16)
 
 
 def local(
@@ -218,7 +230,7 @@
     row_type = jax.ShapeDtypeStruct((half_rows, column_count), jnp.bfloat16)
     hub_type = jax.ShapeDtypeStruct((hub_total, column_count), jnp.bfloat16)
     for group, slots in enumerate(send_order(reach)):
-        hubs = group > 0 and hub_theirs is not None
+        hubs = group % 2 == 1 and hub_theirs is not None
         picked = pl.pallas_call(
             functools.partial(pick_kernel, slots=slots, with_hubs=hubs),
             out_shape=[hub_type] * hubs + [row_type] * len(slots),
@@ -231,11 +243,6 @@
             start_stage()
         for slot, rows in zip(slots, picked[hubs:]):
             received[slot] = passed_along(rows, "dom", offsets[slot])
-    while hub_theirs is not None:
-        hub_mine = hub_mine + hub_theirs
-        start_stage()
-    hub_block = hub_mine
-
     lists = [pltpu.SMEM((tile_values.shape[0] + UNROLL,), jnp.int32)] * 3
     acc_shape = (blocks + 1, edge, column_count)
     partial_sum = pl.pallas_call(
@@ -246,28 +253,45 @@
         scratch_shapes=lists,
         name="own_tiles",
     )(tile_rows, tile_cols, tile_count, tile_values, rows_bf16)
-    sources = received + [hub_block]
-    ext_rows = sum(source.shape[0] for source in sources)
-    return pl.pallas_call(
-        rest_kernel,
-        out_shape=jax.ShapeDtypeStruct((vertex_rows, column_count), jnp.bfloat16),
-        in_specs=[smem] * 3 + [vmem] * 3 + [hbm] * len(sources),
-        out_specs=vmem,
-        scratch_shapes=[
+    while hub_theirs is not None:
+        hub_mine = hub_mine + hub_theirs
+        start_stage()
+
+    ext_rows = vertex_rows + slot_total * half_rows + hub_total
+
+    def add_more(held, arrays, finish):
+        starts = [vertex_rows + slot * half_rows for slot in held]
+        scratch = [
             pltpu.VMEM((ext_rows, column_count), jnp.bfloat16),
-            pltpu.VMEM(acc_shape, jnp.float32),
-            pltpu.SemaphoreType.DMA((len(sources),)),
+            pltpu.SemaphoreType.DMA((len(held),)),
         ]
-        + lists,
-        name="other_tiles",
-    )(
-        tile_rows,
-        tile_cols,
-        tile_count,
-        out_bias.reshape(1, column_count),
-        tile_values,
-        partial_sum,
-        *sources,
+        if finish:
+            shape = jax.ShapeDtypeStruct((vertex_rows, column_count), jnp.bfloat16)
+            scratch.append(pltpu.VMEM(acc_shape, jnp.float32))
+        else:
+            shape = jax.ShapeDtypeStruct(acc_shape, jnp.float32)
+        return pl.pallas_call(
+            functools.partial(more_kernel, starts=starts, finish=finish),
+            out_shape=shape,
+            in_specs=[smem] * 3 + [vmem] * 3 + [hbm] * len(held),
+            out_specs=vmem,
+            scratch_shapes=scratch + lists,
+            name="other_tiles",
+        )(
+            tile_rows,
+            tile_cols,
+            tile_count,
+            out_bias.reshape(1, column_count),
+            tile_values,
+            partial_sum,
+            *arrays,
+        )
+
+    order = [slot for slots in send_order(reach) for slot in slots]
+    early, late = sorted(order[:reach]), sorted(order[reach:])
+    partial_sum = add_more(early, [received[slot] for slot in early], False)
+    return add_more(
+        late + [slot_total], [received[slot] for slot in late] + [hub_mine], True
     )
 
 

time: 83.9 us -> 88.2 us (1.051)
  the two profiles are of different devices: /device:TPU:2 before, /device:TPU:22 now
where the time goes in v1:
time: 88.2 us; the launch traced here: 87.6 us
  Pallas kernels  35 us (40%)
  starting transfers between devices  30.9 us (35%)
  waiting for transfers between devices  11.7 us (13%)
  local copies, waits for them, and re-layouts  6.96 us (8%)
  other arithmetic  2.19 us (2%)
  between operations  0.89 us (1%)
    ppermute x8, starting transfers between devices, passed_along(): lax.ppermute(value, axis, [(source, source + steps) for source in range(i...  27.3 us
    pallas_call x2, Pallas kernels, add_more(): pl.pallas_call(functools.partial(more_kernel, starts=starts, finish=finis...  13.5 us
    pallas_call x4, Pallas kernels, local(): pl.pallas_call(functools.partial(pick_kernel, slots=slots, with_hubs=hubs...  13.1 us
    ppermute x4, waiting for transfers between devices, exchanged(): return lax.ppermute(value, axis, [(i, i ^ step) for i in range(count)])  11.6 us
    pallas_call x1, Pallas kernels, local(): pl.pallas_call(own_kernel, out_shape=jax.ShapeDtypeStruct(acc_shape, jnp....  4.8 us
    unnamed x24, local copies, waits for them, and re-layouts  4.56 us
    ppermute x4, starting transfers between devices, exchanged(): return lax.ppermute(value, axis, [(i, i ^ step) for i in range(count)])  3.65 us
    pallas_call x1, Pallas kernels, local(): pl.pallas_call(functools.partial(project_kernel, parts=feat_size), out_sh...  3.57 us
  transfers between devices with their start and end apart: 13, of which 3 were waited for; matrix products, arithmetic and copies ran while one was open for 5% of the time, Pallas kernels for 28%

profile of v1, /device:TPU:22, one launch (start us, length us, event | category | flops | bytes accessed | tf_op | source)
XLA Modules:
  0.0 87.6 jit_solution(8157681979761465091)
XLA Ops:
  0.0 0.0 collective-permute-start
  0.0 0.7 broadcast_subtract_fusion
  0.7 0.8 copy.10.local_hubs
  1.5 1.6 %fusion = (bf16[304,128]{1,0:T(8,128)(2,1)}, bf16[304,128]{1,0:T(8,128)(2,1)}) fusion(bf16[608,256]{1,0:T(8,128)(2,1)} %param.10, s32[]{:T(128)S(6)} %select_n.25, s32[]{:T(128)S(6)} %select_n.23, s32[]{:T(128)S(6)} %select_n.22), kind=kLoop, calls=%fused_computation.1 | loop fusion | bytes 311308 | tf_op jit(solution)/shard_map/dynamic_slice | solution.py:193
  3.1 0.1 collective-permute-done.refs_1_
  3.2 0.0 copy-start
  3.2 1.1 %copy-done = bf16[304,2048]{1,0:T(8,128)(2,1)} copy-done((bf16[304,2048]{1,0:T(8,128)(2,1)}, bf16[304,2048]{1,0:T(8,128)(2,1)S(1)}, u32[]{:S(2)}) %copy-start) | copy-done | bytes 1245208
  4.2 3.6 %project.1 = (bf16[512,512]{1,0:T(8,128)(2,1)}, bf16[2048,128]{1,0:T(8,128)(2,1)}, bf16[256,128]{1,0:T(8,128)(2,1)}) custom-call(s32[256,1]{1,0:T(8,128)} %copy.10.local_hubs, bf16[304,2048]{1,0:T(8,128)(2,1)} %bitcast.5, bf16[304,2048]{1,0:T(8,128)(2,1)} %copy-done, bf16[304,128]{1,0:T(8,128)(2,1)} %get-tuple-element.32.refs_2_, ...), custom_call_target="tpu_custom_call" | custom-call | tf_op jit(solution)/shard_map/project/pallas_call | solution.py:203
  7.8 0.5 collective-permute-start.1
  8.3 3.3 %pick_rows.5 = (bf16[1024,128]{1,0:T(8,128)(2,1)}, bf16[1024,128]{1,0:T(8,128)(2,1)}) custom-call(s32[8,1024]{1,0:T(8,128)} %bitcast.6, bf16[512,512]{1,0:T(8,128)(2,1)} %get-tuple-element.19.folded), custom_call_target="tpu_custom_call" | custom-call | tf_op jit(solution)/shard_map/pick_rows/pallas_call | solution.py:234
  11.6 4.3 %collective-permute-start.4 = (bf16[1024,128]{1,0:T(8,128)(2,1)}, bf16[1024,128]{1,0:T(8,128)(2,1)S(1)}, u32[]{:S(2)}, u32[]{:S(2)}) collective-permute-start(bf16[1024,128]{1,0:T(8,128)(2,1)} %get-tuple-element.23), channel_id=1, source_target_pairs={{0,2},{2,4},{4,6},{6,8},{8,10},{10,12},{12,14},{14,16},{16,18},{18... | collective-permute-start | bytes 786440 | tf_op jit(solution)/shard_map/ppermute | solution.py:19
  16.0 3.4 %collective-permute-start.5 = (bf16[1024,128]{1,0:T(8,128)(2,1)}, bf16[1024,128]{1,0:T(8,128)(2,1)S(1)}, u32[]{:S(2)}, u32[]{:S(2)}) collective-permute-start(bf16[1024,128]{1,0:T(8,128)(2,1)} %get-tuple-element.24), channel_id=1, source_target_pairs={{0,4},{2,6},{4,8},{6,10},{8,12},{10,14},{12,16},{14,18},{16,20},{1... | collective-permute-start | bytes 786440 | tf_op jit(solution)/shard_map/ppermute | solution.py:19
  19.4 0.0 collective-permute-done.1.refs_1_
  19.4 0.0 copy-start.9
  19.4 0.6 copy-done.9
  20.0 3.3 %pick_rows.4 = (bf16[256,128]{1,0:T(8,128)(2,1)}, bf16[1024,128]{1,0:T(8,128)(2,1)}, bf16[1024,128]{1,0:T(8,128)(2,1)}) custom-call(s32[8,1024]{1,0:T(8,128)} %bitcast.7, bf16[512,512]{1,0:T(8,128)(2,1)} %get-tuple-element.19.folded, bf16[256,128]{1,0:T(8,128)(2,1)} %get-tuple-element.20.refs_0_, bf16[256,128]{1,0:T(8,128)(2,1)} %copy-done.9), custom_call_target="tpu_custom_call" | custom-call | tf_op jit(solution)/shard_map/pick_rows/pallas_call | solution.py:234
  23.3 0.0 copy-start.11
  23.3 2.5 %collective-permute-start.2 = (bf16[1024,128]{1,0:T(8,128)(2,1)}, bf16[1024,128]{1,0:T(8,128)(2,1)S(1)}, u32[]{:S(2)}, u32[]{:S(2)}) collective-permute-start(bf16[1024,128]{1,0:T(8,128)(2,1)} %get-tuple-element.21), channel_id=1, source_target_pairs={{4,0},{6,2},{8,4},{10,6},{12,8},{14,10},{16,12},{18,14},{20,16},{2... | collective-permute-start | bytes 786440 | tf_op jit(solution)/shard_map/ppermute | solution.py:19
  25.9 1.5 %collective-permute-start.6 = (bf16[256,128]{1,0:T(8,128)(2,1)}, bf16[256,128]{1,0:T(8,128)(2,1)S(1)}, u32[]{:S(2)}, u32[]{:S(2)}) collective-permute-start(bf16[256,128]{1,0:T(8,128)(2,1)} %get-tuple-element.25.refs_0_), channel_id=1, source_target_pairs={{0,4},{2,6},{4,0},{6,2},{8,12},{10,14},{12,8},{14,10},{16,20},{18,... | collective-permute-start | bytes 196616 | tf_op jit(solution)/shard_map/ppermute | solution.py:24
  27.3 8.7 %collective-permute-done.6.refs_1_ = bf16[256,128]{1,0:T(8,128)(2,1)S(1)} collective-permute-done((bf16[256,128]{1,0:T(8,128)(2,1)}, bf16[256,128]{1,0:T(8,128)(2,1)S(1)}, u32[]{:S(2)}, u32[]{:S(2)}) %collective-permute-start.6) | collective-permute-done | bytes 65568 | tf_op jit(solution)/shard_map/ppermute | solution.py:24
  36.0 0.0 copy-start.10
  36.0 0.6 copy-done.10
  36.7 3.3 %pick_rows.6 = (bf16[256,128]{1,0:T(8,128)(2,1)}, bf16[1024,128]{1,0:T(8,128)(2,1)}, bf16[1024,128]{1,0:T(8,128)(2,1)}) custom-call(s32[8,1024]{1,0:T(8,128)} %bitcast.8, bf16[512,512]{1,0:T(8,128)(2,1)} %get-tuple-element.19.folded, bf16[256,128]{1,0:T(8,128)(2,1)} %get-tuple-element.25.refs_0_, bf16[256,128]{1,0:T(8,128)(2,1)} %copy-done.10), custom_call_target="tpu_custom_call" | custom-call | tf_op jit(solution)/shard_map/pick_rows/pallas_call | solution.py:234
  39.9 1.6 %collective-permute-start.11 = (bf16[256,128]{1,0:T(8,128)(2,1)}, bf16[256,128]{1,0:T(8,128)(2,1)S(1)}, u32[]{:S(2)}, u32[]{:S(2)}) collective-permute-start(bf16[256,128]{1,0:T(8,128)(2,1)} %get-tuple-element.30), channel_id=1, source_target_pairs={{0,8},{2,10},{4,12},{6,14},{8,0},{10,2},{12,4},{14,6},{16,24},{18,... | collective-permute-start | bytes 196616 | tf_op jit(solution)/shard_map/ppermute | solution.py:24
  41.5 2.9 %collective-permute-done.11 = bf16[256,128]{1,0:T(8,128)(2,1)S(1)} collective-permute-done((bf16[256,128]{1,0:T(8,128)(2,1)}, bf16[256,128]{1,0:T(8,128)(2,1)S(1)}, u32[]{:S(2)}, u32[]{:S(2)}) %collective-permute-start.11) | collective-permute-done | bytes 65568 | tf_op jit(solution)/shard_map/ppermute | solution.py:24
  44.4 0.9 add.29
  45.2 0.1 collective-permute-start.12
  45.3 3.3 %pick_rows.7 = (bf16[1024,128]{1,0:T(8,128)(2,1)}, bf16[1024,128]{1,0:T(8,128)(2,1)}) custom-call(s32[8,1024]{1,0:T(8,128)} %bitcast.9, bf16[512,512]{1,0:T(8,128)(2,1)} %get-tuple-element.19.folded), custom_call_target="tpu_custom_call" | custom-call | tf_op jit(solution)/shard_map/pick_rows/pallas_call | solution.py:234
  48.6 4.3 %collective-permute-start.9 = (bf16[1024,128]{1,0:T(8,128)(2,1)}, bf16[1024,128]{1,0:T(8,128)(2,1)S(1)}, u32[]{:S(2)}, u32[]{:S(2)}) collective-permute-start(bf16[1024,128]{1,0:T(8,128)(2,1)} %get-tuple-element.28), channel_id=1, source_target_pairs={{0,6},{2,8},{4,10},{6,12},{8,14},{10,16},{12,18},{14,20},{16,22},{... | collective-permute-start | bytes 786440 | tf_op jit(solution)/shard_map/ppermute | solution.py:19
  52.9 0.0 collective-permute-done.4.refs_2_
  52.9 0.0 copy-start.1
  52.9 0.0 copy-done.11
  53.0 4.7 %collective-permute-start.3 = (bf16[1024,128]{1,0:T(8,128)(2,1)S(1)}, bf16[1024,128]{1,0:T(8,128)(2,1)S(1)}, u32[]{:S(2)}, u32[]{:S(2)}) collective-permute-start(bf16[1024,128]{1,0:T(8,128)(2,1)S(1)} %copy-done.11), channel_id=1, source_target_pairs={{2,0},{4,2},{6,4},{8,6},{10,8},{12,10},{14,12},{16,14},{18,16},{20... | collective-permute-start | bytes 786440 | tf_op jit(solution)/shard_map/ppermute | solution.py:19
  57.6 0.0 collective-permute-done.5.refs_3_
  57.7 0.0 copy-start.2
  57.7 1.9 %collective-permute-start.10 = (bf16[1024,128]{1,0:T(8,128)(2,1)}, bf16[1024,128]{1,0:T(8,128)(2,1)S(1)}, u32[]{:S(2)}, u32[]{:S(2)}) collective-permute-start(bf16[1024,128]{1,0:T(8,128)(2,1)} %get-tuple-element.29), channel_id=1, source_target_pairs={{0,8},{2,10},{4,12},{6,14},{8,16},{10,18},{12,20},{14,22},{16,24},... | collective-permute-start | bytes 786440 | tf_op jit(solution)/shard_map/ppermute | solution.py:19
  59.6 0.0 collective-permute-done.12
  59.6 3.9 %collective-permute-start.7 = (bf16[1024,128]{1,0:T(8,128)(2,1)}, bf16[1024,128]{1,0:T(8,128)(2,1)S(1)}, u32[]{:S(2)}, u32[]{:S(2)}) collective-permute-start(bf16[1024,128]{1,0:T(8,128)(2,1)} %get-tuple-element.26), channel_id=1, source_target_pairs={{8,0},{10,2},{12,4},{14,6},{16,8},{18,10},{20,12},{22,14},{24,16},... | collective-permute-start | bytes 786440 | tf_op jit(solution)/shard_map/ppermute | solution.py:19
  63.5 0.0 collective-permute-done.2.refs_0_
  63.5 0.0 copy-start.3
  63.6 2.1 %collective-permute-start.8 = (bf16[1024,128]{1,0:T(8,128)(2,1)}, bf16[1024,128]{1,0:T(8,128)(2,1)S(1)}, u32[]{:S(2)}, u32[]{:S(2)}) collective-permute-start(bf16[1024,128]{1,0:T(8,128)(2,1)} %get-tuple-element.27), channel_id=1, source_target_pairs={{6,0},{8,2},{10,4},{12,6},{14,8},{16,10},{18,12},{20,14},{22,16},{... | collective-permute-start | bytes 786440 | tf_op jit(solution)/shard_map/ppermute | solution.py:19
  66.3 4.8 %own_tiles.1.acc_in = f32[17,128,128]{2,1,0:T(8,128)} custom-call(s32[108]{0:T(128)} %rows.5, s32[108]{0:T(128)} %cols.5, s32[1]{0:T(128)S(6)} %copy.11.count, bf16[108,128,128]{2,1,0:T(8,128)(2,1)} %tiles.5, bf16[2048,128]{1,0:T(8,128)(2,1)} %get-tuple-element.18.own), custom_call_target="tpu_custom_call" | custom-call | tf_op jit(solution)/shard_map/own_tiles/pallas_call | solution.py:248
  71.1 0.0 copy-done.1
  71.1 0.0 copy-done.2
  71.1 0.0 copy-done.3
  71.1 0.6 add.30.refs_4_
  71.8 0.0 collective-permute-done.3.refs_1_
  71.8 0.0 copy-start.7
  71.8 0.7 copy-done.7
  72.5 7.0 %other_tiles.2.acc_in = f32[17,128,128]{2,1,0:T(8,128)} custom-call(s32[108]{0:T(128)} %rows.5, s32[108]{0:T(128)} %cols.5, s32[1]{0:T(128)S(6)} %copy.11.count, f32[1,128]{1,0:T(1,128)} %bitcast.11, bf16[108,128,128]{2,1,0:T(8,128)(2,1)} %tiles.5, f32[17,128,128]{2,1,0:T(8,128)} %own_tiles.1.acc_in, bf16[1024,128]{1,0:T(8,128)(2,1)} %copy-done.3, ...), custom_call_target="tpu_custom_call" | custom-call | tf_op jit(solution)/shard_map/other_tiles/pallas_call | solution.py:273
  79.5 0.0 collective-permute-done.9.refs_2_
  79.5 0.0 copy-start.4
  79.5 0.0 collective-permute-done.10.refs_3_
  79.5 0.0 copy-start.5
  79.5 0.0 collective-permute-done.7.refs_0_
  79.5 0.0 copy-start.6
  79.6 0.0 collective-permute-done.8.refs_1_
  79.6 0.6 copy-done.4
  80.2 0.1 copy-done.5
  80.3 0.1 copy-done.6
  80.4 0.0 copy-start.8
  80.4 0.7 copy-done.8
  81.1 6.5 %other_tiles.3 = bf16[2048,128]{1,0:T(8,128)(2,1)} custom-call(s32[108]{0:T(128)} %rows.5, s32[108]{0:T(128)} %cols.5, s32[1]{0:T(128)S(6)} %copy.11.count, f32[1,128]{1,0:T(1,128)} %bitcast.12, bf16[108,128,128]{2,1,0:T(8,128)(2,1)} %tiles.5, f32[17,128,128]{2,1,0:T(8,128)} %other_tiles.2.acc_in, bf16[1024,128]{1,0:T(8,128)(2,1)} %copy-done.6, ...), custom_call_target="tpu_custom_call" | custom-call | tf_op jit(solution)/shard_map/other_tiles/pallas_call | solution.py:273
Async XLA Ops:
  0.0 3.2 %collective-permute-start = (bf16[304,2048]{1,0:T(8,128)(2,1)}, bf16[304,2048]{1,0:T(8,128)(2,1)S(1)}, u32[]{:S(2)}, u32[]{:S(2)}) collective-permute-start(bf16[304,2048]{1,0:T(8,128)(2,1)} %bitcast.4), channel_id=1, source_target_pairs={{0,1},{1,0},{2,3},{3,2},{4,5},{5,4},{6,7},{7,6},{8,9},{9,8},{10,11... | collective-permute-start | bytes 3735560 | tf_op jit(solution)/shard_map/ppermute | solution.py:189
  3.2 1.1 %copy-start = (bf16[304,2048]{1,0:T(8,128)(2,1)}, bf16[304,2048]{1,0:T(8,128)(2,1)S(1)}, u32[]{:S(2)}) copy-start(bf16[304,2048]{1,0:T(8,128)(2,1)S(1)} %collective-permute-done.refs_1_) | copy-start | bytes 3735556
  7.8 11.6 %collective-permute-start.1 = (bf16[256,128]{1,0:T(8,128)(2,1)}, bf16[256,128]{1,0:T(8,128)(2,1)S(1)}, u32[]{:S(2)}, u32[]{:S(2)}) collective-permute-start(bf16[256,128]{1,0:T(8,128)(2,1)} %get-tuple-element.20.refs_0_), channel_id=1, source_target_pairs={{0,2},{2,0},{4,6},{6,4},{8,10},{10,8},{12,14},{14,12},{16,18},{18,... | collective-permute-start | bytes 196616 | tf_op jit(solution)/shard_map/ppermute | solution.py:24
  11.6 41.3 %collective-permute-start.4 = (bf16[1024,128]{1,0:T(8,128)(2,1)}, bf16[1024,128]{1,0:T(8,128)(2,1)S(1)}, u32[]{:S(2)}, u32[]{:S(2)}) collective-permute-start(bf16[1024,128]{1,0:T(8,128)(2,1)} %get-tuple-element.23), channel_id=1, source_target_pairs={{0,2},{2,4},{4,6},{6,8},{8,10},{10,12},{12,14},{14,16},{16,18},{18... | collective-permute-start | bytes 786440 | tf_op jit(solution)/shard_map/ppermute | solution.py:19
  16.0 41.7 %collective-permute-start.5 = (bf16[1024,128]{1,0:T(8,128)(2,1)}, bf16[1024,128]{1,0:T(8,128)(2,1)S(1)}, u32[]{:S(2)}, u32[]{:S(2)}) collective-permute-start(bf16[1024,128]{1,0:T(8,128)(2,1)} %get-tuple-element.24), channel_id=1, source_target_pairs={{0,4},{2,6},{4,8},{6,10},{8,12},{10,14},{12,16},{14,18},{16,20},{1... | collective-permute-start | bytes 786440 | tf_op jit(solution)/shard_map/ppermute | solution.py:19
  19.4 0.6 copy-start.9
  23.3 29.6 %copy-start.11 = (bf16[1024,128]{1,0:T(8,128)(2,1)S(1)}, bf16[1024,128]{1,0:T(8,128)(2,1)}, u32[]{:S(2)}) copy-start(bf16[1024,128]{1,0:T(8,128)(2,1)} %get-tuple-element.22) | copy-start | bytes 786436
  23.3 40.2 %collective-permute-start.2 = (bf16[1024,128]{1,0:T(8,128)(2,1)}, bf16[1024,128]{1,0:T(8,128)(2,1)S(1)}, u32[]{:S(2)}, u32[]{:S(2)}) collective-permute-start(bf16[1024,128]{1,0:T(8,128)(2,1)} %get-tuple-element.21), channel_id=1, source_target_pairs={{4,0},{6,2},{8,4},{10,6},{12,8},{14,10},{16,12},{18,14},{20,16},{2... | collective-permute-start | bytes 786440 | tf_op jit(solution)/shard_map/ppermute | solution.py:19
  25.9 10.2 %collective-permute-start.6 = (bf16[256,128]{1,0:T(8,128)(2,1)}, bf16[256,128]{1,0:T(8,128)(2,1)S(1)}, u32[]{:S(2)}, u32[]{:S(2)}) collective-permute-start(bf16[256,128]{1,0:T(8,128)(2,1)} %get-tuple-element.25.refs_0_), channel_id=1, source_target_pairs={{0,4},{2,6},{4,0},{6,2},{8,12},{10,14},{12,8},{14,10},{16,20},{18,... | collective-permute-start | bytes 196616 | tf_op jit(solution)/shard_map/ppermute | solution.py:24
  36.0 0.6 copy-start.10
  39.9 4.5 %collective-permute-start.11 = (bf16[256,128]{1,0:T(8,128)(2,1)}, bf16[256,128]{1,0:T(8,128)(2,1)S(1)}, u32[]{:S(2)}, u32[]{:S(2)}) collective-permute-start(bf16[256,128]{1,0:T(8,128)(2,1)} %get-tuple-element.30), channel_id=1, source_target_pairs={{0,8},{2,10},{4,12},{6,14},{8,0},{10,2},{12,4},{14,6},{16,24},{18,... | collective-permute-start | bytes 196616 | tf_op jit(solution)/shard_map/ppermute | solution.py:24
  45.2 14.3 %collective-permute-start.12 = (bf16[256,128]{1,0:T(8,128)(2,1)S(1)}, bf16[256,128]{1,0:T(8,128)(2,1)S(1)}, u32[]{:S(2)}, u32[]{:S(2)}) collective-permute-start(bf16[256,128]{1,0:T(8,128)(2,1)S(1)} %add.29), channel_id=1, source_target_pairs={{0,16},{2,18},{4,20},{6,22},{8,24},{10,26},{12,28},{14,30},{16,0},... | collective-permute-start | bytes 196616 | tf_op jit(solution)/shard_map/ppermute | solution.py:24
  48.6 30.9 %collective-permute-start.9 = (bf16[1024,128]{1,0:T(8,128)(2,1)}, bf16[1024,128]{1,0:T(8,128)(2,1)S(1)}, u32[]{:S(2)}, u32[]{:S(2)}) collective-permute-start(bf16[1024,128]{1,0:T(8,128)(2,1)} %get-tuple-element.28), channel_id=1, source_target_pairs={{0,6},{2,8},{4,10},{6,12},{8,14},{10,16},{12,18},{14,20},{16,22},{... | collective-permute-start | bytes 786440 | tf_op jit(solution)/shard_map/ppermute | solution.py:19
  52.9 18.2 %copy-start.1 = (bf16[1024,128]{1,0:T(8,128)(2,1)}, bf16[1024,128]{1,0:T(8,128)(2,1)S(1)}, u32[]{:S(2)}) copy-start(bf16[1024,128]{1,0:T(8,128)(2,1)S(1)} %collective-permute-done.4.refs_2_) | copy-start | bytes 786436
  53.0 18.8 %collective-permute-start.3 = (bf16[1024,128]{1,0:T(8,128)(2,1)S(1)}, bf16[1024,128]{1,0:T(8,128)(2,1)S(1)}, u32[]{:S(2)}, u32[]{:S(2)}) collective-permute-start(bf16[1024,128]{1,0:T(8,128)(2,1)S(1)} %copy-done.11), channel_id=1, source_target_pairs={{2,0},{4,2},{6,4},{8,6},{10,8},{12,10},{14,12},{16,14},{18,16},{20... | collective-permute-start | bytes 786440 | tf_op jit(solution)/shard_map/ppermute | solution.py:19
  57.7 13.5 %copy-start.2 = (bf16[1024,128]{1,0:T(8,128)(2,1)}, bf16[1024,128]{1,0:T(8,128)(2,1)S(1)}, u32[]{:S(2)}) copy-start(bf16[1024,128]{1,0:T(8,128)(2,1)S(1)} %collective-permute-done.5.refs_3_) | copy-start | bytes 786436
  57.7 21.9 %collective-permute-start.10 = (bf16[1024,128]{1,0:T(8,128)(2,1)}, bf16[1024,128]{1,0:T(8,128)(2,1)S(1)}, u32[]{:S(2)}, u32[]{:S(2)}) collective-permute-start(bf16[1024,128]{1,0:T(8,128)(2,1)} %get-tuple-element.29), channel_id=1, source_target_pairs={{0,8},{2,10},{4,12},{6,14},{8,16},{10,18},{12,20},{14,22},{16,24},... | collective-permute-start | bytes 786440 | tf_op jit(solution)/shard_map/ppermute | solution.py:19
  59.6 19.9 %collective-permute-start.7 = (bf16[1024,128]{1,0:T(8,128)(2,1)}, bf16[1024,128]{1,0:T(8,128)(2,1)S(1)}, u32[]{:S(2)}, u32[]{:S(2)}) collective-permute-start(bf16[1024,128]{1,0:T(8,128)(2,1)} %get-tuple-element.26), channel_id=1, source_target_pairs={{8,0},{10,2},{12,4},{14,6},{16,8},{18,10},{20,12},{22,14},{24,16},... | collective-permute-start | bytes 786440 | tf_op jit(solution)/shard_map/ppermute | solution.py:19
  63.5 7.6 %copy-start.3 = (bf16[1024,128]{1,0:T(8,128)(2,1)}, bf16[1024,128]{1,0:T(8,128)(2,1)S(1)}, u32[]{:S(2)}) copy-start(bf16[1024,128]{1,0:T(8,128)(2,1)S(1)} %collective-permute-done.2.refs_0_) | copy-start | bytes 786436
  63.6 16.0 %collective-permute-start.8 = (bf16[1024,128]{1,0:T(8,128)(2,1)}, bf16[1024,128]{1,0:T(8,128)(2,1)S(1)}, u32[]{:S(2)}, u32[]{:S(2)}) collective-permute-start(bf16[1024,128]{1,0:T(8,128)(2,1)} %get-tuple-element.27), channel_id=1, source_target_pairs={{6,0},{8,2},{10,4},{12,6},{14,8},{16,10},{18,12},{20,14},{22,16},{... | collective-permute-start | bytes 786440 | tf_op jit(solution)/shard_map/ppermute | solution.py:19
  71.8 0.7 copy-start.7
  79.5 0.7 copy-start.4
  79.5 0.8 copy-start.5
  79.5 0.9 copy-start.6
  80.4 0.7 copy-start.8

commit v2 on v0

--- a/solution.py
+++ b/solution.py
@@ -10,7 +10,7 @@
 
 UNROLL = 4
 FOLDS = 4
-ORDER = ((5, 4), (2, 3), (6, 7), (1, 0))
+ORDER = ((5, 4, 2, 3), (6, 7, 1, 0))
 
 
 def passed_along(value, axis, steps):
@@ -27,7 +27,8 @@
 def send_order(reach):
     if reach == 4:
         return ORDER
-    return tuple((k, 2 * reach - 1 - k) for k in range(reach))
+    near = [slot for k in range(reach) for slot in (reach + k, reach - 1 - k)]
+    return tuple(near[:reach]), tuple(near[reach:])
 
 
 def project_kernel(local_hubs, *refs, parts):
@@ -79,37 +80,50 @@
             out[start : start + piece] = picked.astype(jnp.bfloat16)
 
 
-def listed(rows, cols, count, chosen, first, last, spare):
-    chosen_slot, chosen_row, chosen_col = chosen
+def fetched(rows, cols, count, tiles, lists, ranges, spare):
+    held, sems, chosen_row, chosen_col = lists
 
     def step(t, n):
         col = cols[t]
-        chosen_slot[n] = t
         chosen_row[n] = rows[t]
         chosen_col[n] = col
-        return n + jnp.where((col >= first) & (col < last), 1, 0)
+        inside = (col >= ranges[0][0]) & (col < ranges[0][1])
+        for first, last in ranges[1:]:
+            inside |= (col >= first) & (col < last)
+
+        @pl.when(inside)
+        def _():
+            pltpu.make_async_copy(tiles.at[t], held.at[n], sems.at[n]).start()
+
+        return n + jnp.where(inside, 1, 0)
 
     n = lax.fori_loop(0, count[0], step, jnp.int32(0))
     for j in range(UNROLL):
-        chosen_slot[n + j] = 0
         chosen_row[n + j] = spare
-        chosen_col[n + j] = first
+        chosen_col[n + j] = ranges[0][0]
     return n
 
 
-def add_products(n, chosen, tiles, ext, base, acc):
-    chosen_slot, chosen_row, chosen_col = chosen
-    edge = tiles.shape[1]
+def add_products(n, tiles, lists, ext, acc):
+    held, sems, chosen_row, chosen_col = lists
+    edge = held.shape[1]
 
     @pl.loop(0, (n + UNROLL - 1) // UNROLL)
     def _(group):
         products = []
         for j in range(UNROLL):
             k = group * UNROLL + j
-            start = pl.multiple_of((chosen_col[k] - base) * edge, edge)
+
+            @pl.when(k < n)
+            def _():
+                pltpu.make_async_copy(tiles.at[0], held.at[k], sems.at[k]).wait()
+
+        for j in range(UNROLL):
+            k = group * UNROLL + j
+            start = pl.multiple_of(chosen_col[k] * edge, edge)
             products.append(
                 jnp.dot(
-                    tiles[chosen_slot[k]],
+                    held[jnp.minimum(k, n - 1)],
                     ext[pl.ds(start, edge), :],
                     preferred_element_type=jnp.float32,
                 )
@@ -119,32 +133,33 @@
             acc[row] += products[j]
 
 
-def own_kernel(rows, cols, count, tiles, own, acc, *chosen):
+def own_kernel(rows, cols, count, tiles, own, acc, *lists):
     blocks = acc.shape[0] - 1
+    n = fetched(rows, cols, count, tiles, lists, ((0, blocks),), blocks)
     acc[...] = jnp.zeros(acc.shape, jnp.float32)
-    n = listed(rows, cols, count, chosen, 0, own.shape[0] // tiles.shape[1], blocks)
-    add_products(n, chosen, tiles, own, 0, acc)
+    add_products(n, tiles, lists, own, acc)
 
 
 def rest_kernel(rows, cols, count, bias, tiles, acc_in, *refs):
-    sources = refs[:-7]
-    out, ext, acc, sems = refs[-7:-3]
-    chosen = refs[-3:]
+    sources = refs[:-8]
+    out, ext, acc, source_sems = refs[-8:-4]
+    lists = refs[-4:]
     edge = tiles.shape[1]
-    copies, start = [], 0
+    blocks = acc.shape[0] - 1
+    copies, start = [], blocks * edge
     for k, source in enumerate(sources):
         copies.append(
-            pltpu.make_async_copy(source, ext.at[pl.ds(start, source.shape[0]), :], sems.at[k])
+            pltpu.make_async_copy(
+                source, ext.at[pl.ds(start, source.shape[0]), :], source_sems.at[k]
+            )
         )
         start += source.shape[0]
         copies[-1].start()
-    blocks = acc.shape[0] - 1
-    first = blocks
+    n = fetched(rows, cols, count, tiles, lists, ((blocks, start // edge),), blocks)
     acc[...] = acc_in[...]
-    n = listed(rows, cols, count, chosen, first, first + start // edge, blocks)
     for copy in copies:
         copy.wait()
-    add_products(n, chosen, tiles, ext, first, acc)
+    add_products(n, tiles, lists, ext, acc)
     total = acc[:blocks].reshape(out.shape)
     out[...] = jnp.maximum(total + bias[...], 0.0).astype(jnp.bfloat16)
 
@@ -218,7 +233,7 @@
     row_type = jax.ShapeDtypeStruct((half_rows, column_count), jnp.bfloat16)
     hub_type = jax.ShapeDtypeStruct((hub_total, column_count), jnp.bfloat16)
     for group, slots in enumerate(send_order(reach)):
-        hubs = group > 0 and hub_theirs is not None
+        hubs = group % 2 == 1 and hub_theirs is not None
         picked = pl.pallas_call(
             functools.partial(pick_kernel, slots=slots, with_hubs=hubs),
             out_shape=[hub_type] * hubs + [row_type] * len(slots),
@@ -231,27 +246,31 @@
             start_stage()
         for slot, rows in zip(slots, picked[hubs:]):
             received[slot] = passed_along(rows, "dom", offsets[slot])
-    while hub_theirs is not None:
-        hub_mine = hub_mine + hub_theirs
-        start_stage()
-    hub_block = hub_mine
-
-    lists = [pltpu.SMEM((tile_values.shape[0] + UNROLL,), jnp.int32)] * 3
+    tile_slots = tile_values.shape[0]
+    lists = [
+        pltpu.VMEM(tile_values.shape, tile_values.dtype),
+        pltpu.SemaphoreType.DMA((tile_slots,)),
+        pltpu.SMEM((tile_slots + UNROLL,), jnp.int32),
+        pltpu.SMEM((tile_slots + UNROLL,), jnp.int32),
+    ]
     acc_shape = (blocks + 1, edge, column_count)
     partial_sum = pl.pallas_call(
         own_kernel,
         out_shape=jax.ShapeDtypeStruct(acc_shape, jnp.float32),
-        in_specs=[smem] * 3 + [vmem] * 2,
+        in_specs=[smem] * 3 + [hbm, vmem],
         out_specs=vmem,
         scratch_shapes=lists,
         name="own_tiles",
     )(tile_rows, tile_cols, tile_count, tile_values, rows_bf16)
-    sources = received + [hub_block]
-    ext_rows = sum(source.shape[0] for source in sources)
+    while hub_theirs is not None:
+        hub_mine = hub_mine + hub_theirs
+        start_stage()
+    sources = received + [hub_mine]
+    ext_rows = vertex_rows + sum(source.shape[0] for source in sources)
     return pl.pallas_call(
         rest_kernel,
         out_shape=jax.ShapeDtypeStruct((vertex_rows, column_count), jnp.bfloat16),
-        in_specs=[smem] * 3 + [vmem] * 3 + [hbm] * len(sources),
+        in_specs=[smem] * 3 + [vmem, hbm, vmem] + [hbm] * len(sources),
         out_specs=vmem,
         scratch_shapes=[
             pltpu.VMEM((ext_rows, column_count), jnp.bfloat16),

time: 83.9 us -> 75 us (0.89)
  the two profiles are of different devices: /device:TPU:2 before, /device:TPU:20 now
where the time goes in v2:
time: 75 us; the launch traced here: 74.4 us
  starting transfers between devices  29.3 us (39%)
  Pallas kernels  22.8 us (30%)
  waiting for transfers between devices  14.3 us (19%)
  local copies, waits for them, and re-layouts  4.83 us (6%)
  other arithmetic  2.22 us (3%)
  between operations  0.9 us (1%)
    ppermute x8, starting transfers between devices, passed_along(): lax.ppermute(value, axis, [(source, source + steps) for source in range(i...  24.6 us
    pallas_call x2, Pallas kernels, local(): pl.pallas_call(functools.partial(pick_kernel, slots=slots, with_hubs=hubs...  8.79 us
    ppermute x4, waiting for transfers between devices, exchanged(): return lax.ppermute(value, axis, [(i, i ^ step) for i in range(count)])  8.47 us
    pallas_call x1, Pallas kernels, local(): pl.pallas_call(rest_kernel, out_shape=jax.ShapeDtypeStruct((vertex_rows,...  6.22 us
    ppermute x8, waiting for transfers between devices, passed_along(): lax.ppermute(value, axis, [(source, source + steps) for source in range(i...  5.75 us
    ppermute x4, starting transfers between devices, exchanged(): return lax.ppermute(value, axis, [(i, i ^ step) for i in range(count)])  4.66 us
    pallas_call x1, Pallas kernels, local(): pl.pallas_call(own_kernel, out_shape=jax.ShapeDtypeStruct(acc_shape, jnp....  4.25 us
    pallas_call x1, Pallas kernels, local(): pl.pallas_call(functools.partial(project_kernel, parts=feat_size), out_sh...  3.56 us
  transfers between devices with their start and end apart: 13, of which 4 were waited for; matrix products, arithmetic and copies ran while one was open for 6% of the time, Pallas kernels for 12%

profile of v2, /device:TPU:20, one launch (start us, length us, event | category | flops | bytes accessed | tf_op | source)
XLA Modules:
  0.0 74.4 jit_solution(4229667329506157332)
XLA Ops:
  0.0 0.0 collective-permute-start
  0.0 0.7 broadcast_subtract_fusion
  0.7 0.8 %copy.10.local_hubs = s32[256,1]{1,0:T(8,128)} copy(s32[256,1]{0,1:T(1,128)S(1)} %bitcast.8) | data formatting | bytes 2048 | tf_op jit(solution)/shard_map/reshape | solution.py:202
  1.5 1.6 %fusion = (bf16[304,128]{1,0:T(8,128)(2,1)}, bf16[304,128]{1,0:T(8,128)(2,1)}) fusion(bf16[608,256]{1,0:T(8,128)(2,1)} %param.10, s32[]{:T(128)S(6)} %select_n.25, s32[]{:T(128)S(6)} %select_n.23, s32[]{:T(128)S(6)} %select_n.22), kind=kLoop, calls=%fused_computation.1 | loop fusion | bytes 311308 | tf_op jit(solution)/shard_map/dynamic_slice | solution.py:196
  3.1 0.1 collective-permute-done.refs_1_
  3.2 0.0 copy-start
  3.2 1.1 %copy-done = bf16[304,2048]{1,0:T(8,128)(2,1)} copy-done((bf16[304,2048]{1,0:T(8,128)(2,1)}, bf16[304,2048]{1,0:T(8,128)(2,1)S(1)}, u32[]{:S(2)}) %copy-start) | copy-done | bytes 1245208
  4.3 3.6 %project.1 = (bf16[512,512]{1,0:T(8,128)(2,1)}, bf16[2048,128]{1,0:T(8,128)(2,1)}, bf16[256,128]{1,0:T(8,128)(2,1)}) custom-call(s32[256,1]{1,0:T(8,128)} %copy.10.local_hubs, bf16[304,2048]{1,0:T(8,128)(2,1)} %bitcast.5, bf16[304,2048]{1,0:T(8,128)(2,1)} %copy-done, bf16[304,128]{1,0:T(8,128)(2,1)} %get-tuple-element.30.refs_2_, ...), custom_call_target="tpu_custom_call" | custom-call | tf_op jit(solution)/shard_map/project/pallas_call | solution.py:206
  7.8 4.4 %pick_rows.3 = (bf16[1024,128]{1,0:T(8,128)(2,1)}, bf16[1024,128]{1,0:T(8,128)(2,1)}, bf16[1024,128]{1,0:T(8,128)(2,1)}, bf16[1024,128]{1,0:T(8,128)(2,1)}) custom-call(s32[8,1024]{1,0:T(8,128)} %bitcast.6, bf16[512,512]{1,0:T(8,128)(2,1)} %get-tuple-element.18.folded), custom_call_target="tpu_custom_call" | custom-call | tf_op jit(solution)/shard_map/pick_rows/pallas_call | solution.py:237
  12.2 2.4 %collective-permute-start.4 = (bf16[1024,128]{1,0:T(8,128)(2,1)}, bf16[1024,128]{1,0:T(8,128)(2,1)S(1)}, u32[]{:S(2)}, u32[]{:S(2)}) collective-permute-start(bf16[1024,128]{1,0:T(8,128)(2,1)} %get-tuple-element.22), channel_id=1, source_target_pairs={{4,0},{6,2},{8,4},{10,6},{12,8},{14,10},{16,12},{18,14},{20,16},{2... | collective-permute-start | bytes 786440 | tf_op jit(solution)/shard_map/ppermute | solution.py:19
  14.6 1.6 %collective-permute-start.1 = (bf16[256,128]{1,0:T(8,128)(2,1)}, bf16[256,128]{1,0:T(8,128)(2,1)S(1)}, u32[]{:S(2)}, u32[]{:S(2)}) collective-permute-start(bf16[256,128]{1,0:T(8,128)(2,1)} %get-tuple-element.19.refs_0_), channel_id=1, source_target_pairs={{0,2},{2,0},{4,6},{6,4},{8,10},{10,8},{12,14},{14,12},{16,18},{18,... | collective-permute-start | bytes 196616 | tf_op jit(solution)/shard_map/ppermute | solution.py:24
  16.2 3.3 %collective-permute-start.5 = (bf16[1024,128]{1,0:T(8,128)(2,1)}, bf16[1024,128]{1,0:T(8,128)(2,1)S(1)}, u32[]{:S(2)}, u32[]{:S(2)}) collective-permute-start(bf16[1024,128]{1,0:T(8,128)(2,1)} %get-tuple-element.23), channel_id=1, source_target_pairs={{2,0},{4,2},{6,4},{8,6},{10,8},{12,10},{14,12},{16,14},{18,16},{20... | collective-permute-start | bytes 786440 | tf_op jit(solution)/shard_map/ppermute | solution.py:19
  19.5 2.6 %collective-permute-start.6 = (bf16[1024,128]{1,0:T(8,128)(2,1)}, bf16[1024,128]{1,0:T(8,128)(2,1)S(1)}, u32[]{:S(2)}, u32[]{:S(2)}) collective-permute-start(bf16[1024,128]{1,0:T(8,128)(2,1)} %get-tuple-element.24), channel_id=1, source_target_pairs={{0,2},{2,4},{4,6},{6,8},{8,10},{10,12},{12,14},{14,16},{16,18},{18... | collective-permute-start | bytes 786440 | tf_op jit(solution)/shard_map/ppermute | solution.py:19
  22.0 0.0 collective-permute-done.1.refs_1_
  22.0 0.0 copy-start.9
  22.0 0.6 copy-done.9
  22.7 4.4 %pick_rows.2 = (bf16[256,128]{1,0:T(8,128)(2,1)}, bf16[1024,128]{1,0:T(8,128)(2,1)}, bf16[1024,128]{1,0:T(8,128)(2,1)}, bf16[1024,128]{1,0:T(8,128)(2,1)}, bf16[1024,128]{1,0:T(8,128)(2,1)}) custom-call(s32[8,1024]{1,0:T(8,128)} %bitcast.7, bf16[512,512]{1,0:T(8,128)(2,1)} %get-tuple-element.18.folded, bf16[256,128]{1,0:T(8,128)(2,1)} %get-tuple-element.19.refs_0_, ...), custom_call_target="tpu_custom_call" | custom-call | tf_op jit(solution)/shard_map/pick_rows/pallas_call | solution.py:237
  27.1 1.4 %collective-permute-start.10 = (bf16[256,128]{1,0:T(8,128)(2,1)}, bf16[256,128]{1,0:T(8,128)(2,1)S(1)}, u32[]{:S(2)}, u32[]{:S(2)}) collective-permute-start(bf16[256,128]{1,0:T(8,128)(2,1)} %get-tuple-element.28), channel_id=1, source_target_pairs={{0,4},{2,6},{4,0},{6,2},{8,12},{10,14},{12,8},{14,10},{16,20},{18,... | collective-permute-start | bytes 196616 | tf_op jit(solution)/shard_map/ppermute | solution.py:24
  28.4 5.8 %collective-permute-done.10 = bf16[256,128]{1,0:T(8,128)(2,1)S(1)} collective-permute-done((bf16[256,128]{1,0:T(8,128)(2,1)}, bf16[256,128]{1,0:T(8,128)(2,1)S(1)}, u32[]{:S(2)}, u32[]{:S(2)}) %collective-permute-start.10) | collective-permute-done | bytes 65568 | tf_op jit(solution)/shard_map/ppermute | solution.py:24
  34.2 0.9 %add.32 = bf16[256,128]{1,0:T(8,128)(2,1)S(1)} add(bf16[256,128]{1,0:T(8,128)(2,1)} %get-tuple-element.28, bf16[256,128]{1,0:T(8,128)(2,1)S(1)} %collective-permute-done.10) | non-fusion elementwise | flops 32768 | bytes 196608 | tf_op jit(solution)/shard_map/add | solution.py:266
  35.1 1.6 %collective-permute-start.11 = (bf16[256,128]{1,0:T(8,128)(2,1)S(1)}, bf16[256,128]{1,0:T(8,128)(2,1)S(1)}, u32[]{:S(2)}, u32[]{:S(2)}) collective-permute-start(bf16[256,128]{1,0:T(8,128)(2,1)S(1)} %add.32), channel_id=1, source_target_pairs={{0,8},{2,10},{4,12},{6,14},{8,0},{10,2},{12,4},{14,6},{16,24},{18,... | collective-permute-start | bytes 196616 | tf_op jit(solution)/shard_map/ppermute | solution.py:24
  36.7 2.7 %collective-permute-done.11 = bf16[256,128]{1,0:T(8,128)(2,1)S(1)} collective-permute-done((bf16[256,128]{1,0:T(8,128)(2,1)S(1)}, bf16[256,128]{1,0:T(8,128)(2,1)S(1)}, u32[]{:S(2)}, u32[]{:S(2)}) %collective-permute-start.11) | collective-permute-done | bytes 65568 | tf_op jit(solution)/shard_map/ppermute | solution.py:24
  39.4 0.1 collective-permute-start.12
  39.5 2.9 %collective-permute-start.7 = (bf16[1024,128]{1,0:T(8,128)(2,1)}, bf16[1024,128]{1,0:T(8,128)(2,1)S(1)}, u32[]{:S(2)}, u32[]{:S(2)}) collective-permute-start(bf16[1024,128]{1,0:T(8,128)(2,1)} %get-tuple-element.25), channel_id=1, source_target_pairs={{0,4},{2,6},{4,8},{6,10},{8,12},{10,14},{12,16},{14,18},{16,20},{1... | collective-permute-start | bytes 786440 | tf_op jit(solution)/shard_map/ppermute | solution.py:19
  42.4 0.0 collective-permute-done.4.refs_2_
  42.4 0.0 copy-start.1
  42.4 4.0 %collective-permute-start.2 = (bf16[1024,128]{1,0:T(8,128)(2,1)}, bf16[1024,128]{1,0:T(8,128)(2,1)S(1)}, u32[]{:S(2)}, u32[]{:S(2)}) collective-permute-start(bf16[1024,128]{1,0:T(8,128)(2,1)} %get-tuple-element.20), channel_id=1, source_target_pairs={{8,0},{10,2},{12,4},{14,6},{16,8},{18,10},{20,12},{22,14},{24,16},... | collective-permute-start | bytes 786440 | tf_op jit(solution)/shard_map/ppermute | solution.py:19
  46.4 0.0 collective-permute-done.5.refs_3_
  46.4 0.0 copy-start.2
  46.4 2.9 %collective-permute-start.3 = (bf16[1024,128]{1,0:T(8,128)(2,1)}, bf16[1024,128]{1,0:T(8,128)(2,1)S(1)}, u32[]{:S(2)}, u32[]{:S(2)}) collective-permute-start(bf16[1024,128]{1,0:T(8,128)(2,1)} %get-tuple-element.21), channel_id=1, source_target_pairs={{6,0},{8,2},{10,4},{12,6},{14,8},{16,10},{18,12},{20,14},{22,16},{... | collective-permute-start | bytes 786440 | tf_op jit(solution)/shard_map/ppermute | solution.py:19
  49.4 0.0 collective-permute-done.6.refs_4_
  49.4 0.0 copy-start.3
  49.4 4.7 %collective-permute-start.8 = (bf16[1024,128]{1,0:T(8,128)(2,1)}, bf16[1024,128]{1,0:T(8,128)(2,1)S(1)}, u32[]{:S(2)}, u32[]{:S(2)}) collective-permute-start(bf16[1024,128]{1,0:T(8,128)(2,1)} %get-tuple-element.26), channel_id=1, source_target_pairs={{0,6},{2,8},{4,10},{6,12},{8,14},{10,16},{12,18},{14,20},{16,22},{... | collective-permute-start | bytes 786440 | tf_op jit(solution)/shard_map/ppermute | solution.py:19
  54.1 0.0 collective-permute-done.12
  54.1 1.9 %collective-permute-start.9 = (bf16[1024,128]{1,0:T(8,128)(2,1)}, bf16[1024,128]{1,0:T(8,128)(2,1)S(1)}, u32[]{:S(2)}, u32[]{:S(2)}) collective-permute-start(bf16[1024,128]{1,0:T(8,128)(2,1)} %get-tuple-element.27), channel_id=1, source_target_pairs={{0,8},{2,10},{4,12},{6,14},{8,16},{10,18},{12,20},{14,22},{16,24},... | collective-permute-start | bytes 786440 | tf_op jit(solution)/shard_map/ppermute | solution.py:19
  56.7 4.2 %own_tiles.1.acc_in = f32[17,128,128]{2,1,0:T(8,128)} custom-call(s32[108]{0:T(128)} %rows.3, s32[108]{0:T(128)} %cols.3, s32[1]{0:T(128)S(6)} %copy.11.count, bf16[108,128,128]{2,1,0:T(8,128)(2,1)} %tiles.3, bf16[2048,128]{1,0:T(8,128)(2,1)} %get-tuple-element.17.own), custom_call_target="tpu_custom_call" | custom-call | tf_op jit(solution)/shard_map/own_tiles/pallas_call | solution.py:257
  61.0 0.0 copy-done.1
  61.0 0.0 copy-done.2
  61.0 0.0 copy-done.3
  61.0 0.7 add.34.refs_8_
  61.6 0.0 collective-permute-done.7.refs_5_
  61.6 0.0 copy-start.4
  61.6 0.0 collective-permute-done.2.refs_0_
  61.6 0.0 copy-start.5
  61.7 0.0 collective-permute-done.3.refs_1_
  61.7 0.0 copy-start.6
  61.7 0.0 collective-permute-done.8.refs_6_
  61.7 0.0 copy-start.7
  61.7 5.7 %collective-permute-done.9.refs_7_ = bf16[1024,128]{1,0:T(8,128)(2,1)S(1)} collective-permute-done((bf16[1024,128]{1,0:T(8,128)(2,1)}, bf16[1024,128]{1,0:T(8,128)(2,1)S(1)}, u32[]{:S(2)}, u32[]{:S(2)}) %collective-permute-start.9) | collective-permute-done | bytes 262176 | tf_op jit(solution)/shard_map/ppermute | solution.py:19
  67.4 0.0 copy-start.8
  67.4 0.0 copy-done.4
  67.4 0.0 copy-done.5
  67.4 0.0 copy-done.6
  67.4 0.0 copy-done.7
  67.5 0.7 copy-done.8
  68.1 6.2 %other_tiles.1 = bf16[2048,128]{1,0:T(8,128)(2,1)} custom-call(s32[108]{0:T(128)} %rows.3, s32[108]{0:T(128)} %cols.3, s32[1]{0:T(128)S(6)} %copy.11.count, f32[1,128]{1,0:T(1,128)} %bitcast.9, bf16[108,128,128]{2,1,0:T(8,128)(2,1)} %tiles.3, f32[17,128,128]{2,1,0:T(8,128)} %own_tiles.1.acc_in, bf16[1024,128]{1,0:T(8,128)(2,1)} %copy-done.5, ...), custom_call_target="tpu_custom_call" | custom-call | tf_op jit(solution)/shard_map/other_tiles/pallas_call | solution.py:270
  (1 shorter events, 0.0 us)
Async XLA Ops:
  0.0 3.2 %collective-permute-start = (bf16[304,2048]{1,0:T(8,128)(2,1)}, bf16[304,2048]{1,0:T(8,128)(2,1)S(1)}, u32[]{:S(2)}, u32[]{:S(2)}) collective-permute-start(bf16[304,2048]{1,0:T(8,128)(2,1)} %bitcast.4), channel_id=1, source_target_pairs={{0,1},{1,0},{2,3},{3,2},{4,5},{5,4},{6,7},{7,6},{8,9},{9,8},{10,11... | collective-permute-start | bytes 3735560 | tf_op jit(solution)/shard_map/ppermute | solution.py:192
  3.2 1.1 %copy-start = (bf16[304,2048]{1,0:T(8,128)(2,1)}, bf16[304,2048]{1,0:T(8,128)(2,1)S(1)}, u32[]{:S(2)}) copy-start(bf16[304,2048]{1,0:T(8,128)(2,1)S(1)} %collective-permute-done.refs_1_) | copy-start | bytes 3735556
  12.2 30.2 %collective-permute-start.4 = (bf16[1024,128]{1,0:T(8,128)(2,1)}, bf16[1024,128]{1,0:T(8,128)(2,1)S(1)}, u32[]{:S(2)}, u32[]{:S(2)}) collective-permute-start(bf16[1024,128]{1,0:T(8,128)(2,1)} %get-tuple-element.22), channel_id=1, source_target_pairs={{4,0},{6,2},{8,4},{10,6},{12,8},{14,10},{16,12},{18,14},{20,16},{2... | collective-permute-start | bytes 786440 | tf_op jit(solution)/shard_map/ppermute | solution.py:19
  14.6 7.4 %collective-permute-start.1 = (bf16[256,128]{1,0:T(8,128)(2,1)}, bf16[256,128]{1,0:T(8,128)(2,1)S(1)}, u32[]{:S(2)}, u32[]{:S(2)}) collective-permute-start(bf16[256,128]{1,0:T(8,128)(2,1)} %get-tuple-element.19.refs_0_), channel_id=1, source_target_pairs={{0,2},{2,0},{4,6},{6,4},{8,10},{10,8},{12,14},{14,12},{16,18},{18,... | collective-permute-start | bytes 196616 | tf_op jit(solution)/shard_map/ppermute | solution.py:24
  16.2 30.2 %collective-permute-start.5 = (bf16[1024,128]{1,0:T(8,128)(2,1)}, bf16[1024,128]{1,0:T(8,128)(2,1)S(1)}, u32[]{:S(2)}, u32[]{:S(2)}) collective-permute-start(bf16[1024,128]{1,0:T(8,128)(2,1)} %get-tuple-element.23), channel_id=1, source_target_pairs={{2,0},{4,2},{6,4},{8,6},{10,8},{12,10},{14,12},{16,14},{18,16},{20... | collective-permute-start | bytes 786440 | tf_op jit(solution)/shard_map/ppermute | solution.py:19
  19.5 29.9 %collective-permute-start.6 = (bf16[1024,128]{1,0:T(8,128)(2,1)}, bf16[1024,128]{1,0:T(8,128)(2,1)S(1)}, u32[]{:S(2)}, u32[]{:S(2)}) collective-permute-start(bf16[1024,128]{1,0:T(8,128)(2,1)} %get-tuple-element.24), channel_id=1, source_target_pairs={{0,2},{2,4},{4,6},{6,8},{8,10},{10,12},{12,14},{14,16},{16,18},{18... | collective-permute-start | bytes 786440 | tf_op jit(solution)/shard_map/ppermute | solution.py:19
  22.0 0.6 copy-start.9
  27.1 7.2 %collective-permute-start.10 = (bf16[256,128]{1,0:T(8,128)(2,1)}, bf16[256,128]{1,0:T(8,128)(2,1)S(1)}, u32[]{:S(2)}, u32[]{:S(2)}) collective-permute-start(bf16[256,128]{1,0:T(8,128)(2,1)} %get-tuple-element.28), channel_id=1, source_target_pairs={{0,4},{2,6},{4,0},{6,2},{8,12},{10,14},{12,8},{14,10},{16,20},{18,... | collective-permute-start | bytes 196616 | tf_op jit(solution)/shard_map/ppermute | solution.py:24
  35.1 4.3 %collective-permute-start.11 = (bf16[256,128]{1,0:T(8,128)(2,1)S(1)}, bf16[256,128]{1,0:T(8,128)(2,1)S(1)}, u32[]{:S(2)}, u32[]{:S(2)}) collective-permute-start(bf16[256,128]{1,0:T(8,128)(2,1)S(1)} %add.32), channel_id=1, source_target_pairs={{0,8},{2,10},{4,12},{6,14},{8,0},{10,2},{12,4},{14,6},{16,24},{18,... | collective-permute-start | bytes 196616 | tf_op jit(solution)/shard_map/ppermute | solution.py:24
  39.4 14.7 %collective-permute-start.12 = (bf16[256,128]{1,0:T(8,128)(2,1)S(1)}, bf16[256,128]{1,0:T(8,128)(2,1)S(1)}, u32[]{:S(2)}, u32[]{:S(2)}) collective-permute-start(bf16[256,128]{1,0:T(8,128)(2,1)S(1)} %add.33), channel_id=1, source_target_pairs={{0,16},{2,18},{4,20},{6,22},{8,24},{10,26},{12,28},{14,30},{16,0},... | collective-permute-start | bytes 196616 | tf_op jit(solution)/shard_map/ppermute | solution.py:24
  39.5 22.1 %collective-permute-start.7 = (bf16[1024,128]{1,0:T(8,128)(2,1)}, bf16[1024,128]{1,0:T(8,128)(2,1)S(1)}, u32[]{:S(2)}, u32[]{:S(2)}) collective-permute-start(bf16[1024,128]{1,0:T(8,128)(2,1)} %get-tuple-element.25), channel_id=1, source_target_pairs={{0,4},{2,6},{4,8},{6,10},{8,12},{10,14},{12,16},{14,18},{16,20},{1... | collective-permute-start | bytes 786440 | tf_op jit(solution)/shard_map/ppermute | solution.py:19
  42.4 18.5 %copy-start.1 = (bf16[1024,128]{1,0:T(8,128)(2,1)}, bf16[1024,128]{1,0:T(8,128)(2,1)S(1)}, u32[]{:S(2)}) copy-start(bf16[1024,128]{1,0:T(8,128)(2,1)S(1)} %collective-permute-done.4.refs_2_) | copy-start | bytes 786436
  42.4 19.2 %collective-permute-start.2 = (bf16[1024,128]{1,0:T(8,128)(2,1)}, bf16[1024,128]{1,0:T(8,128)(2,1)S(1)}, u32[]{:S(2)}, u32[]{:S(2)}) collective-permute-start(bf16[1024,128]{1,0:T(8,128)(2,1)} %get-tuple-element.20), channel_id=1, source_target_pairs={{8,0},{10,2},{12,4},{14,6},{16,8},{18,10},{20,12},{22,14},{24,16},... | collective-permute-start | bytes 786440 | tf_op jit(solution)/shard_map/ppermute | solution.py:19
  46.4 14.6 %copy-start.2 = (bf16[1024,128]{1,0:T(8,128)(2,1)}, bf16[1024,128]{1,0:T(8,128)(2,1)S(1)}, u32[]{:S(2)}) copy-start(bf16[1024,128]{1,0:T(8,128)(2,1)S(1)} %collective-permute-done.5.refs_3_) | copy-start | bytes 786436
  46.4 15.2 %collective-permute-start.3 = (bf16[1024,128]{1,0:T(8,128)(2,1)}, bf16[1024,128]{1,0:T(8,128)(2,1)S(1)}, u32[]{:S(2)}, u32[]{:S(2)}) collective-permute-start(bf16[1024,128]{1,0:T(8,128)(2,1)} %get-tuple-element.21), channel_id=1, source_target_pairs={{6,0},{8,2},{10,4},{12,6},{14,8},{16,10},{18,12},{20,14},{22,16},{... | collective-permute-start | bytes 786440 | tf_op jit(solution)/shard_map/ppermute | solution.py:19
  49.4 11.6 %copy-start.3 = (bf16[1024,128]{1,0:T(8,128)(2,1)}, bf16[1024,128]{1,0:T(8,128)(2,1)S(1)}, u32[]{:S(2)}) copy-start(bf16[1024,128]{1,0:T(8,128)(2,1)S(1)} %collective-permute-done.6.refs_4_) | copy-start | bytes 786436
  49.4 12.3 %collective-permute-start.8 = (bf16[1024,128]{1,0:T(8,128)(2,1)}, bf16[1024,128]{1,0:T(8,128)(2,1)S(1)}, u32[]{:S(2)}, u32[]{:S(2)}) collective-permute-start(bf16[1024,128]{1,0:T(8,128)(2,1)} %get-tuple-element.26), channel_id=1, source_target_pairs={{0,6},{2,8},{4,10},{6,12},{8,14},{10,16},{12,18},{14,20},{16,22},{... | collective-permute-start | bytes 786440 | tf_op jit(solution)/shard_map/ppermute | solution.py:19
  54.1 13.3 %collective-permute-start.9 = (bf16[1024,128]{1,0:T(8,128)(2,1)}, bf16[1024,128]{1,0:T(8,128)(2,1)S(1)}, u32[]{:S(2)}, u32[]{:S(2)}) collective-permute-start(bf16[1024,128]{1,0:T(8,128)(2,1)} %get-tuple-element.27), channel_id=1, source_target_pairs={{0,8},{2,10},{4,12},{6,14},{8,16},{10,18},{12,20},{14,22},{16,24},... | collective-permute-start | bytes 786440 | tf_op jit(solution)/shard_map/ppermute | solution.py:19
  61.6 5.8 %copy-start.4 = (bf16[1024,128]{1,0:T(8,128)(2,1)}, bf16[1024,128]{1,0:T(8,128)(2,1)S(1)}, u32[]{:S(2)}) copy-start(bf16[1024,128]{1,0:T(8,128)(2,1)S(1)} %collective-permute-done.7.refs_5_) | copy-start | bytes 786436
  61.6 5.8 %copy-start.5 = (bf16[1024,128]{1,0:T(8,128)(2,1)}, bf16[1024,128]{1,0:T(8,128)(2,1)S(1)}, u32[]{:S(2)}) copy-start(bf16[1024,128]{1,0:T(8,128)(2,1)S(1)} %collective-permute-done.2.refs_0_) | copy-start | bytes 786436
  61.7 5.8 %copy-start.6 = (bf16[1024,128]{1,0:T(8,128)(2,1)}, bf16[1024,128]{1,0:T(8,128)(2,1)S(1)}, u32[]{:S(2)}) copy-start(bf16[1024,128]{1,0:T(8,128)(2,1)S(1)} %collective-permute-done.3.refs_1_) | copy-start | bytes 786436
  61.7 5.8 %copy-start.7 = (bf16[1024,128]{1,0:T(8,128)(2,1)}, bf16[1024,128]{1,0:T(8,128)(2,1)S(1)}, u32[]{:S(2)}) copy-start(bf16[1024,128]{1,0:T(8,128)(2,1)S(1)} %collective-permute-done.8.refs_6_) | copy-start | bytes 786436
  67.4 0.7 copy-start.8
